TPU v7x, 256 devices: a 4x2x16 block of a 4x16x16 slice. The times are simulated.
256 devices in a mesh: groups: 2 (over y), expert: 32 (over z, core), tensor: 4 (over x).
Axes of the slice: x: 4, y: 2, z: 16, core: 2. Of those that a mesh axis runs over, the one named last changes fastest.
The devices are a block of a 4x16x16 slice.
Arguments:
- tokens: bfloat16 [8192, 6144], P(('groups', 'expert', 'tensor')), parts along dimension 0, may hold values from -6 to 6
- expert_ids: int32 [8192, 2], P(('groups', 'expert', 'tensor')), parts along dimension 0, may hold values from 0 to 31, all different within a row; in each aligned block of 32 rows (0 to 31, 32 to 63, ...) at most 4 rows name the same one
- gate_scores: float32 [8192, 2], P(('groups', 'expert', 'tensor')), parts along dimension 0, may hold values from 0.1 to 1
- norm_gain: float32 [6144], replicated, may hold values from 0.1 to 1.9
- w_gate: bfloat16 [32, 6144, 1024], P('expert', None, 'tensor'), may hold values from -0.078125 to 0.078125
- w_up: bfloat16 [32, 6144, 1024], P('expert', None, 'tensor'), may hold values from -0.078125 to 0.078125
- w_down: bfloat16 [32, 1024, 6144], P('expert', 'tensor'), may hold values from -0.1875 to 0.1875
Outputs:
- mixed: bfloat16 [8192, 6144], P(('groups', 'expert', 'tensor')), parts along dimension 0
There are 2 independent parts, one for each index of `groups`. A program takes and returns all parts, laid end to end along the dimension named above; an argument that names none is the same for every part. Nothing has to cross between parts.
Inputs may be any that keep to these rules, and one draw needn't show every extreme that they name: `expert_ids`: each token names 2 different experts. Within the 32 tokens of one device, no expert is named more than 4 times, a bound that some block reaches.
All inputs are finite; a program needn't handle non-finite values.
Results may differ from a plain program's by a relative error of at most 0.011.
Values may be sent and summed in bfloat16 or wider, within the bound.
A program may use at most 64 MiB of HBM per device.

v0:
```python
import jax
import jax.numpy as jnp
from jax import lax
from jax.sharding import PartitionSpec as P


def on_device(tokens, expert_ids, gate_scores, norm_gain, w_gate, w_up, w_down):
    rows = tokens.shape[0]
    width = tokens.shape[1]
    picks = expert_ids.shape[1]
    experts = lax.axis_size("expert")
    capacity = 4 * rows // experts
    values = tokens.astype(jnp.float32)
    scale = lax.rsqrt(jnp.mean(values * values, axis=-1, keepdims=True) + 1e-05)
    normed = (values * scale * norm_gain).astype(jnp.bfloat16)
    flat_ids = expert_ids.reshape(-1)
    onehot = (flat_ids[:, None] == jnp.arange(experts, dtype=jnp.int32)[None, :]).astype(jnp.int32)
    earlier = jnp.cumsum(onehot, axis=0) - onehot
    slot = jnp.sum(earlier * onehot, axis=1)
    target = flat_ids * capacity + slot
    placing = jnp.arange(experts * capacity, dtype=jnp.int32)[:, None] == target[None, :]
    placing = placing.reshape(experts * capacity, rows, picks)
    place_tok = jnp.sum(placing.astype(jnp.float32), axis=2).astype(jnp.bfloat16)
    weighting = jnp.sum(placing.astype(jnp.float32) * gate_scores[None, :, :], axis=2)
    outgoing = jnp.dot(place_tok, normed, preferred_element_type=jnp.float32).astype(jnp.bfloat16)
    outgoing = outgoing.reshape(experts, capacity, width)
    arrived = lax.all_to_all(outgoing, "expert", split_axis=0, concat_axis=0, tiled=True)
    arrived = arrived.reshape(-1, width)
    piece = lax.all_gather(arrived, "tensor", axis=0, tiled=True)
    gate = jnp.dot(piece, w_gate[0], preferred_element_type=jnp.float32)
    up = jnp.dot(piece, w_up[0], preferred_element_type=jnp.float32)
    hidden = (jax.nn.silu(gate) * up).astype(jnp.bfloat16)
    parts = jnp.dot(hidden, w_down[0], preferred_element_type=jnp.float32)
    summed = lax.psum_scatter(parts.astype(jnp.bfloat16), "tensor", scatter_dimension=0, tiled=True)
    summed = summed.reshape(experts, capacity, width)
    results = lax.all_to_all(summed, "expert", split_axis=0, concat_axis=0, tiled=True)
    results = results.reshape(experts * capacity, width)
    mixed = jnp.dot(weighting.T, results.astype(jnp.float32), preferred_element_type=jnp.float32)
    return mixed.astype(jnp.bfloat16)


def solution(mesh):
    return jax.shard_map(
        on_device,
        mesh=mesh,
        in_specs=(
            P(("groups", "expert", "tensor"), None),
            P(("groups", "expert", "tensor"), None),
            P(("groups", "expert", "tensor"), None),
            P(),
            P("expert", None, "tensor"),
            P("expert", None, "tensor"),
            P("expert", "tensor", None),
        ),
        out_specs=P(("groups", "expert", "tensor"), None),
        check_vma=False,
    )
```

profile of v0, /device:TPU:33, one launch (start us, length us, event | category | flops | bytes accessed | tf_op | source)
XLA Modules:
  0.0 381.0 jit_solution(17998000077517687781)
XLA Ops:
  6.6 1.3 fusion.11
  7.9 0.8 copy.20
  8.7 0.1 eq.30
  8.8 0.1 fusion.17
  8.8 0.1 reduce_window_sum.11
  8.9 0.2 select_reduce_fusion.1
  9.1 0.1 reduce_sum.39
  9.2 0.1 copy.21
  9.3 0.7 multiply_add_fusion
  10.0 0.8 convert_reduce_fusion
  10.8 2.8 convolution_convert_fusion.1
  13.6 3.8 reshape.41
  17.4 103.9 %all_to_all.10 = bf16[32,4,6144]{2,1,0:T(4,128)(2,1)} all-to-all(bf16[32,4,6144]{2,1,0:T(4,128)(2,1)} %reshape.41), channel_id=1, replica_groups=mesh['groups'=2,'expert'=32,'tensor'=4] {'expert'}, dimensions={0} | all-to-all | bytes 3145728 | tf_op jit(solution)/shard_map/all_to_all | solution.py:27
  121.2 3.6 reshape.42
  125.0 63.8 %all-gather.2.cloned.1.call-done = bf16[512,6144]{1,0:T(8,128)(2,1)} async-done(((bf16[128,6144]{1,0:T(8,128)(2,1)}), bf16[512,6144]{1,0:T(8,128)(2,1)}) %all-gather.2.cloned.1.call-update) | async-done | bytes 6291472 | tf_op jit(solution)/shard_map/all_gather | solution.py:29
  188.8 5.6 %fusion.3 = f32[512,256]{1,0:T(8,128)S(1)} fusion(bf16[512,6144]{1,0:T(8,128)(2,1)} %all-gather.2.cloned.1.call-done, bf16[1,6144,256]{2,1,0:T(8,128)(2,1)} %param.11), kind=kOutput, calls=%fused_computation.6 | convolution fusion | flops 1610612736 | bytes 9961472 | tf_op jit(solution)/shard_map/dot_general | solution.py:30
  194.5 0.8 copy-done.2
  195.3 1.8 fusion.8
  197.1 4.5 %convolution_convert_fusion = bf16[512,6144]{1,0:T(8,128)(2,1)} fusion(bf16[512,256]{1,0:T(8,128)(2,1)S(1)} %fusion.8, bf16[1,256,6144]{2,1,0:T(8,128)(2,1)S(1)} %copy-done), kind=kOutput, calls=%fused_computation | convolution fusion | flops 1613758464 | bytes 9699328 | tf_op jit(solution)/shard_map/dot_general | solution.py:33
  201.6 71.0 %reduce-scatter.2.cloned.1.call-done = bf16[128,6144]{1,0:T(8,128)(2,1)} async-done(((bf16[512,6144]{1,0:T(8,128)(2,1)}), bf16[128,6144]{1,0:T(8,128)(2,1)}) %reduce-scatter.2.cloned.1.call-update) | async-done | bytes 1572880 | tf_op jit(solution)/shard_map/reduce_scatter | solution.py:34
  272.6 3.8 reshape.43
  276.4 91.6 %all_to_all.11 = bf16[32,4,6144]{2,1,0:T(4,128)(2,1)} all-to-all(bf16[32,4,6144]{2,1,0:T(4,128)(2,1)} %reshape.43), channel_id=1, replica_groups=mesh['groups'=2,'expert'=32,'tensor'=4] {'expert'}, dimensions={0} | all-to-all | bytes 3145728 | tf_op jit(solution)/shard_map/all_to_all | solution.py:36
  368.0 3.7 reshape.44
  371.6 2.5 fusion.19
  (10 shorter events, 0.2 us)
Async XLA Ops:
  6.5 190.5 %copy-start = (bf16[1,256,6144]{2,1,0:T(8,128)(2,1)S(1)}, bf16[1,256,6144]{2,1,0:T(8,128)(2,1)}, u32[]{:S(2)}) copy-start(bf16[1,256,6144]{2,1,0:T(8,128)(2,1)} %param.13) | copy-start | bytes 9437188
  6.6 182.3 %all-gather.2.cloned.1.call-start = ((), (), s32[]{:S(2)}) async-start(), calls=%async_computation.3 | async-start | bytes 7864320 | tf_op jit(solution)/shard_map/all_gather | solution.py:29
  124.9 147.7 %reduce-scatter.2.cloned.1.call-start = ((), (), s32[]{:S(2)}) async-start(), calls=%async_computation.4 | async-start | bytes 7864320 | tf_op jit(solution)/shard_map/reduce_scatter | solution.py:34
  188.8 5.7 %copy-start.1 = (bf16[512,6144]{1,0:T(8,128)(2,1)S(1)}, bf16[512,6144]{1,0:T(8,128)(2,1)}, u32[]{:S(2)}) copy-start(bf16[512,6144]{1,0:T(8,128)(2,1)} %all-gather.2.cloned.1.call-done) | copy-start | bytes 18874372
  188.8 6.4 %copy-start.2 = (bf16[1,6144,256]{2,1,0:T(8,128)(2,1)S(1)}, bf16[1,6144,256]{2,1,0:T(8,128)(2,1)}, u32[]{:S(2)}) copy-start(bf16[1,6144,256]{2,1,0:T(8,128)(2,1)} %param.12) | copy-start | bytes 9437188
Sparse Core Ops, SparseCore 0:
  125.0 63.7 all-gather.1
  201.7 70.8 reduce-scatter.1
where the time goes:
time: 382 us; the launch traced here: 381 us
  blocking collectives  195 us (51%)
  waiting for transfers between devices  135 us (35%)
  matrix products  17.2 us (5%)
  local copies, waits for them, and re-layouts  16.7 us (4%)
  between operations  13.5 us (4%)
    all_to_all x1, blocking collectives, on_device(): lax.all_to_all(outgoing, 'expert', split_axis=0, concat_axis=0, tiled=True)  104 us
    all_to_all x1, blocking collectives, on_device(): lax.all_to_all(summed, 'expert', split_axis=0, concat_axis=0, tiled=True)  91.6 us
    reduce_scatter x1, waiting for transfers between devices, on_device(): lax.psum_scatter(parts.astype(jnp.bfloat16), 'tensor', scatter_dimension=...  71 us
    all_gather x1, waiting for transfers between devices, on_device(): piece = lax.all_gather(arrived, 'tensor', axis=0, tiled=True)  63.8 us
  transfers between devices with their start and end apart: 2, of which 2 were waited for; matrix products, arithmetic and copies ran while one was open for 0% of the time, Pallas kernels for 0%

commit v1 on v0

v1 whole, which is shorter than its diff:
```python
import functools

import jax
import jax.numpy as jnp
from jax import lax
from jax.experimental import pallas as pl
from jax.experimental.pallas import tpu as pltpu
from jax.sharding import PartitionSpec as P

MESH = pl.DeviceIdType.MESH
F32, BF16 = jnp.float32, jnp.bfloat16
PARTS = 3
DMA = pltpu.SemaphoreType.DMA


def kernel(E, NX, rows, width, norm, meta, wg_in, wu_in, wd_in, out,
           T, M, FS, G, WG, WU, WD, ACC, HID, PB, OPP, RX, R, FR, C, CP, CR, RZ,
           wsem, zs, zr, ps, pr, zms, zmr, pms, pmr, fs, fr, xs, xr, xfs, xfr,
           os_, or_, ms_, mr_, bs, br, cs_, cr_, rs, rr):
    Z = E // 2
    HOP = Z // 4
    cap = 4 * rows // E
    blk = 2 * cap
    fw = width // PARTS
    hid = WG.shape[1]
    e = lax.axis_index("expert")
    x = lax.axis_index("tensor")
    c = lax.rem(e, 2)
    sgn = (1, -1)

    def at_z(k):
        return {"expert": lax.rem(e + 2 * k + 2 * E, E)}

    partner = {"expert": e + 1 - 2 * c}
    side_dev = ({"tensor": lax.rem(x + 1, NX)}, {"tensor": lax.rem(x + NX - 1, NX)})

    def cols(f):
        return pl.ds(pl.multiple_of(f * fw, fw), fw)

    def rcopy(src, dst, s, r, dev):
        return pltpu.make_async_remote_copy(src_ref=src, dst_ref=dst, send_sem=s, recv_sem=r,
                                            device_id=dev, device_id_type=MESH)

    def each_part(body):
        def step(f, carry):
            body(f)
            return carry
        lax.fori_loop(0, PARTS, step, 0)

    def idx(d, j):
        return 0 if j == 0 else 2 * j - 1 + d

    def z_meta(d, j):
        return rcopy(meta if j == 0 else M.at[idx(d, j), 0], M.at[idx(d, j + 1), 0],
                     zms.at[d, j], zmr.at[d, j], at_z(sgn[d]))

    def p_meta(o):
        return rcopy(meta if o == 0 else M.at[o, 0], M.at[o, 1], pms.at[o], pmr.at[o], partner)

    def z_tok(d, j, f):
        src = norm.at[:, cols(f)] if j == 0 else T.at[idx(d, j), 0, :, cols(f)]
        return rcopy(src, T.at[idx(d, j + 1), 0, :, cols(f)], zs.at[d, j, f], zr.at[d, j, f], at_z(sgn[d]))

    def p_tok(o, f):
        src = norm.at[:, cols(f)] if o == 0 else T.at[o, 0, :, cols(f)]
        return rcopy(src, T.at[o, 1, :, cols(f)], ps.at[o, f], pr.at[o, f], partner)

    def far(d, i, f):
        if i == HOP:
            return rcopy(FS.at[c, i - 1, :, cols(f)], G.at[0, Z - 1, :, cols(f)],
                         fs.at[0, i - 1, f], fr.at[0, i - 1, f],
                         {"expert": lax.rem(e + 2 * i * (1 - 2 * c) + 2 * E, E)})
        return rcopy(FS.at[d, i - 1, :, cols(f)], G.at[0, idx(d, HOP + i), :, cols(f)],
                     fs.at[d, i - 1, f], fr.at[d, i - 1, f], at_z(sgn[d] * i))

    groups = [(0, 3)] + [(2 * j - 1, 2 * j + 1) for j in range(2, 2 * HOP - 1)] + [(Z - 3, Z)]
    NG = len(groups)

    def half(g, side):
        b0, b1 = groups[g]
        cut = b0 + 2 if g == 0 else b0 + 1
        return slice(b0, cut) if side == 0 else slice(cut, b1)

    def xsend(g, side):
        b = slice(*groups[g])
        return rcopy(G.at[0, b], G.at[1 + side, b], xs.at[g, side], xr.at[g, side], side_dev[side])

    def xfwd(g, side):
        b = half(g, side)
        return rcopy(G.at[1 + side, b], G.at[3, b], xfs.at[g, side], xfr.at[g, side], side_dev[side])

    def opp(g, side):
        b = half(g, side)
        return rcopy(PB.at[3, b], OPP.at[b], os_.at[g, side], or_.at[g, side], side_dev[side])

    def main(g, side):
        b = slice(*groups[g])
        return rcopy(PB.at[2 - side, b], RX.at[side, b], ms_.at[g, side], mr_.at[g, side], side_dev[side])

    def back(d, i):
        if i == HOP:
            return rcopy(R.at[Z - 1], FR.at[c, i - 1], bs.at[0, i - 1], br.at[0, i - 1],
                         {"expert": lax.rem(e - 2 * i * (1 - 2 * c) + 2 * E, E)})
        return rcopy(R.at[idx(d, HOP + i)], FR.at[d, i - 1], bs.at[d, i - 1], br.at[d, i - 1],
                     at_z(-sgn[d] * i))

    def p_con(o, f):
        return rcopy(CP.at[o, :, cols(f)], CR.at[o, :, cols(f)], cs_.at[o, f], cr_.at[o, f], partner)

    def ring(d, j, f):
        return rcopy(C.at[idx(d, j), :, cols(f)], RZ.at[d, j - 1, :, cols(f)],
                     rs.at[d, j - 1, f], rr.at[d, j - 1, f], at_z(-sgn[d]))

    lane = lax.broadcasted_iota(jnp.int32, (1, 128), 1)

    def picks(o, n, first, scored):
        def both(r):
            return jnp.where(lane < rows, M[o, 0, r:r + 1, :], M[o, 1, r:r + 1, :])
        r = lax.broadcasted_iota(jnp.int32, (n * blk, 128), 0)
        ln = lax.broadcasted_iota(jnp.int32, (n * blk, 128), 1)
        ex = first(r // blk)
        ex = jnp.where(ex >= E, ex - E, ex)
        ex = jnp.where(ex < 0, ex + E, ex)
        slot = (cap * ex + lax.rem(r, cap)).astype(F32)
        mine = (lax.rem(r, blk) // cap) == (ln // rows)
        one = jnp.ones((n * blk, 128), F32)
        a, b = (both(2), both(3)) if scored else (one, one)
        val = jnp.where(both(0) == slot, a, 0.0) + jnp.where(both(1) == slot, b, 0.0)
        return jnp.where(mine, val, 0.0)[:, :2 * rows].astype(BF16)

    def own(o, scored):
        return picks(o, 1, lambda i: i + e, scored)

    def beyond(o, d, scored):
        return picks(o, HOP, lambda i: e + 2 * sgn[d] * (i + 1), scored)

    def select(lhs, o, f):
        return jnp.dot(lhs, T[o, :, :, cols(f)].reshape(2 * rows, fw), preferred_element_type=F32)

    def ffn_in(b0, b1):
        n = NX * (b1 - b0) * blk
        kc = width // 6
        ACC[:, 0:n] = jnp.zeros((2, n, hid), F32)

        def step(k, carry):
            ks = pl.ds(pl.multiple_of(k * kc, kc), kc)
            lhs = G[:, b0:b1, :, ks].reshape(n, kc)
            ACC[0, 0:n] += jnp.dot(lhs, WG[ks, :], preferred_element_type=F32)
            ACC[1, 0:n] += jnp.dot(lhs, WU[ks, :], preferred_element_type=F32)
            return carry
        lax.fori_loop(0, 6, step, 0)
        gate = ACC[0, 0:n]
        h = gate / (1.0 + jnp.exp(-gate)) * ACC[1, 0:n]
        HID[:, b0:b1] = h.astype(BF16).reshape(NX, b1 - b0, blk, hid)

    def ffn_out(g):
        b0, b1 = groups[g]
        n = NX * (b1 - b0) * blk
        kc = width // 6
        lhs = HID[:, b0:b1].reshape(n, hid)

        def step(k, carry):
            ks = pl.ds(pl.multiple_of(k * kc, kc), kc)
            PB[:, b0:b1, :, ks] = jnp.dot(lhs, WD[:, ks], preferred_element_type=F32).astype(BF16).reshape(NX, b1 - b0, blk, kc)
            return carry
        lax.fori_loop(0, 6, step, 0)

    weights = [pltpu.make_async_copy(wg_in.at[0], WG, wsem.at[0]),
               pltpu.make_async_copy(wu_in.at[0], WU, wsem.at[1]),
               pltpu.make_async_copy(wd_in.at[0], WD, wsem.at[2])]
    for w in weights:
        w.start()
    barrier = pltpu.get_barrier_semaphore()
    peers = [at_z(s * k) for k in range(1, HOP + 1) for s in sgn] + list(side_dev) + [partner]
    for dev in peers:
        pl.semaphore_signal(barrier, inc=1, device_id=dev, device_id_type=MESH)
    T[0, 0] = norm[...]
    M[0, 0] = meta[...]
    FR[1 - c, HOP - 1] = jnp.zeros((blk, width), BF16)
    pl.semaphore_wait(barrier, len(peers))

    sent = []

    def go(make, *a):
        make(*a).start()
        sent.append((make, a, False))

    def note(make, *a):
        sent.append((make, a, True))

    for d in (0, 1):
        go(z_meta, d, 0)
    go(p_meta, 0)

    def first(f):
        p_tok(0, f).start()
        z_tok(0, 0, f).start()
        z_tok(1, 0, f).start()
    each_part(first)
    note(p_tok, 0)
    note(z_tok, 0, 0)
    note(z_tok, 1, 0)

    p_meta(0).wait_recv()
    lhs0 = own(0, False)

    def sel0(f):
        p_tok(0, f).wait_recv()
        G[0, 0, :, cols(f)] = select(lhs0, 0, f).astype(BF16)
    each_part(sel0)

    def spread(g):
        go(xsend, g, 0)
        go(xsend, g, 1)

    def forward(g):
        for side in (0, 1):
            xsend(g, side).wait_recv()
            go(xfwd, g, side)

    def gathered(g):
        for side in (0, 1):
            xfwd(g, side).wait_recv()

    for j in range(1, HOP + 1):
        for d in (0, 1):
            z_meta(d, j - 1).wait_recv()
            if j < HOP:
                go(z_meta, d, j)
            go(p_meta, idx(d, j))

        def hop(f):
            for d in (0, 1):
                z_tok(d, j - 1, f).wait_recv()
                if j < HOP:
                    z_tok(d, j, f).start()
                p_tok(idx(d, j), f).start()
        each_part(hop)
        for d in (0, 1):
            if j < HOP:
                note(z_tok, d, j)
            note(p_tok, idx(d, j))
        for d in (0, 1):
            p_meta(idx(d, j)).wait_recv()
        lhs = [own(idx(d, j), False) for d in (0, 1)]
        if j == HOP:
            lhs = [jnp.concatenate([lhs[d], beyond(idx(d, j), d, False)], axis=0) for d in (0, 1)]

        def sel(f):
            for d in (0, 1):
                o = idx(d, j)
                p_tok(o, f).wait_recv()
                got = select(lhs[d], o, f).astype(BF16)
                G[0, o, :, cols(f)] = got[:blk]
                if j == HOP:
                    FS[d, :, :, cols(f)] = got[blk:].reshape(HOP, blk, fw)
            if j == HOP:
                for i in range(1, HOP):
                    for d in (0, 1):
                        far(d, i, f).start()
                far(0, HOP, f).start()
        each_part(sel)
        if j == HOP:
            for i in range(1, HOP):
                for d in (0, 1):
                    note(far, d, i)
            note(far, 0, HOP)
        spread(j - 1)
        if j > 1:
            forward(j - 2)

    for w in weights:
        w.wait()
    gathered(0)
    gathered(1)
    ffn_in(0, 5)
    for i in range(1, HOP):
        for d in (0, 1):
            each_part(lambda f: far(d, i, f).wait_recv())
        if i == HOP - 1:
            each_part(lambda f: far(0, HOP, f).wait_recv())
        spread(HOP + i - 1)
        forward(HOP + i - 2)
        if i == 2:
            gathered(2)
            gathered(3)
            ffn_in(5, 9)
    forward(NG - 1)
    gathered(4)
    gathered(5)
    ffn_in(9, 13)

    def begin(g):
        ffn_out(g)
        go(opp, g, 0)
        go(opp, g, 1)

    def middle(g):
        for side in (0, 1):
            b = half(g, side)
            n = b.stop - b.start
            opp(g, side).wait_recv()

            def add(f):
                PB[2 - side, b, :, cols(f)] = (PB[2 - side, b, :, cols(f)].astype(F32) + OPP[b, :, cols(f)].astype(F32)).astype(BF16)
            each_part(add)
            go(main, g, side)

    def finish(g):
        b = slice(*groups[g])
        for side in (0, 1):
            main(g, side).wait_recv()

        def add(f):
            R[b, :, cols(f)] = (PB[0, b, :, cols(f)].astype(F32) + RX[0, b, :, cols(f)].astype(F32)
                                + RX[1, b, :, cols(f)].astype(F32)).astype(BF16)
        each_part(add)

    def far_back(g):
        i = g - HOP + 1
        for d in (0, 1):
            go(back, d, i)
        if g == NG - 1:
            go(back, 0, HOP)

    def weigh(lhs, rhs):
        return lax.dot_general(lhs, rhs, (((0,), (0,)), ((), ())), preferred_element_type=F32)

    def give(j):
        for d in ((0, 1) if j > 0 else (0,)):
            o = idx(d, j)
            w_own = own(o, True)
            w_far = None
            if j == HOP:
                w_far = beyond(o, d, True)
                for i in range(1, HOP):
                    back(d, i).wait_recv()
                if d == 0:
                    back(0, HOP).wait_recv()

            def step(f):
                u = weigh(w_own, R[o, :, cols(f)])
                if j == HOP:
                    u = u + weigh(w_far, FR[d, :, :, cols(f)].reshape(HOP * blk, fw))
                C[o, :, cols(f)] = u[:rows].astype(BF16)
                CP[o, :, cols(f)] = u[rows:].astype(BF16)
                p_con(o, f).start()
            each_part(step)
            note(p_con, o)

    def pass_on(j):
        def step(f):
            for d in (0, 1):
                o = idx(d, j)
                p_con(o, f).wait_recv()
                v = C[o, :, cols(f)].astype(F32) + CR[o, :, cols(f)].astype(F32)
                if j < HOP:
                    ring(d, j + 1, f).wait_recv()
                    v = v + RZ[d, j, :, cols(f)].astype(F32)
                C[o, :, cols(f)] = v.astype(BF16)
                ring(d, j, f).start()
        each_part(step)
        note(ring, 0, j)
        note(ring, 1, j)

    begin(4)
    begin(5)
    gathered(6)
    ffn_in(13, 16)
    begin(6)
    middle(4)
    middle(5)
    begin(3)
    middle(6)
    finish(4)
    far_back(4)
    finish(5)
    far_back(5)
    middle(3)
    finish(6)
    far_back(6)
    begin(2)
    finish(3)
    middle(2)
    begin(1)
    give(4)
    pass_on(4)
    finish(2)
    give(3)
    middle(1)
    begin(0)
    pass_on(3)
    finish(1)
    give(2)
    middle(0)
    pass_on(2)
    finish(0)
    give(1)
    give(0)
    pass_on(1)

    def last(f):
        p_con(0, f).wait_recv()
        ring(0, 1, f).wait_recv()
        ring(1, 1, f).wait_recv()
        out[:, cols(f)] = (C[0, :, cols(f)].astype(F32) + CR[0, :, cols(f)].astype(F32)
                           + RZ[0, 0, :, cols(f)].astype(F32) + RZ[1, 0, :, cols(f)].astype(F32)).astype(BF16)
    each_part(last)

    for make, a, looped in sent:
        if looped:
            each_part(lambda f: make(*a, f).wait_send())
        else:
            make(*a).wait_send()


def on_device(tokens, expert_ids, gate_scores, norm_gain, w_gate, w_up, w_down):
    rows, width = tokens.shape
    E, NX = lax.axis_size("expert"), lax.axis_size("tensor")
    cap = 4 * rows // E
    Z, HOP, blk, hid = E // 2, E // 8, 2 * cap, w_gate.shape[2]
    values = tokens.astype(F32)
    scale = lax.rsqrt(jnp.mean(values * values, axis=-1, keepdims=True) + 1e-05)
    normed = (values * scale * norm_gain).astype(BF16)
    flat = expert_ids.reshape(-1)
    n = flat.shape[0]
    order = jnp.arange(n, dtype=jnp.int32)
    same = (flat[:, None] == flat[None, :]) & (order[None, :] < order[:, None])
    target = (flat * cap + jnp.sum(same.astype(jnp.int32), axis=1)).reshape(rows, -1).astype(F32)
    info = jnp.concatenate([target.T, gate_scores.T], axis=0)
    info = jnp.concatenate([info, info], axis=1)
    meta = jnp.full((8, 128), -1.0, F32).at[:4, :2 * rows].set(info)
    NG, NO = 2 * HOP - 1, 2 * HOP + 1
    v = lambda *s: pltpu.VMEM(s, BF16)
    return pl.pallas_call(
        functools.partial(kernel, E, NX, rows, width),
        out_shape=jax.ShapeDtypeStruct((rows, width), BF16),
        in_specs=[pl.BlockSpec(memory_space=pltpu.VMEM)] * 2 + [pl.BlockSpec(memory_space=pl.ANY)] * 3,
        out_specs=pl.BlockSpec(memory_space=pltpu.VMEM),
        scratch_shapes=[
            v(NO, 2, rows, width),
            pltpu.VMEM((NO, 2, 8, 128), F32),
            v(2, HOP, blk, width),
            v(NX, Z, blk, width),
            v(width, hid), v(width, hid), v(hid, width),
            pltpu.VMEM((2, NX * 5 * blk, hid), F32),
            v(NX, Z, blk, hid),
            v(NX, Z, blk, width),
            v(Z, blk, width),
            v(2, Z, blk, width),
            v(Z, blk, width),
            v(2, HOP, blk, width),
            v(NO, rows, width), v(NO, rows, width), v(NO, rows, width),
            v(2, HOP, rows, width),
            DMA((3,)),
            DMA((2, HOP, PARTS)), DMA((2, HOP, PARTS)), DMA((NO, PARTS)), DMA((NO, PARTS)),
            DMA((2, HOP)), DMA((2, HOP)), DMA((NO,)), DMA((NO,)),
            DMA((2, HOP, PARTS)), DMA((2, HOP, PARTS)),
            DMA((NG, 2)), DMA((NG, 2)), DMA((NG, 2)), DMA((NG, 2)),
            DMA((NG, 2)), DMA((NG, 2)), DMA((NG, 2)), DMA((NG, 2)),
            DMA((2, HOP)), DMA((2, HOP)),
            DMA((NO, PARTS)), DMA((NO, PARTS)),
            DMA((2, HOP, PARTS)), DMA((2, HOP, PARTS)),
        ],
        compiler_params=pltpu.CompilerParams(collective_id=0, has_side_effects=True, vmem_limit_bytes=63 * 1024 * 1024),
    )(normed, meta, w_gate, w_up, w_down)


def solution(mesh):
    return jax.shard_map(
        on_device,
        mesh=mesh,
        in_specs=(
            P(("groups", "expert", "tensor"), None),
            P(("groups", "expert", "tensor"), None),
            P(("groups", "expert", "tensor"), None),
            P(),
            P("expert", None, "tensor"),
            P("expert", None, "tensor"),
            P("expert", "tensor", None),
        ),
        out_specs=P(("groups", "expert", "tensor"), None),
        check_vma=False,
    )
```

time: 382 us -> 197 us (0.52)
  blocking collectives: 195 us -> 0 us
  Pallas kernels: 0 us -> 189 us
  waiting for transfers between devices: 135 us -> 0 us
  matrix products: 17.2 us -> 0 us
  local copies, waits for them, and re-layouts: 16.7 us -> 2.82 us
  between operations: 13.5 us -> 0.03 us
    all_to_all x2 -> x0, blocking collectives: 195 us -> none  [the longest x1 104 us: on_device(): lax.all_to_all(outgoing, 'expert', split_axis=0, concat_axis=0, tiled=True)]
    pallas_call x0 -> x1, Pallas kernels: none -> 189 us  [on_device(): pl.pallas_call(functools.partial(kernel, E, NX, rows, width), out_shape=j...]
    reduce_scatter x1 -> x0, waiting for transfers between devices: 71 us -> none  [on_device(): lax.psum_scatter(parts.astype(jnp.bfloat16), 'tensor', scatter_dimension=...]
    all_gather x1 -> x0, waiting for transfers between devices: 63.8 us -> none  [on_device(): piece = lax.all_gather(arrived, 'tensor', axis=0, tiled=True)]
    dot_general x5 -> x0, matrix products: 17.2 us -> none  [the longest x1 5.64 us: on_device(): gate = jnp.dot(piece, w_gate[0], preferred_element_type=jnp.float32)]
    reshape x4 -> x0, local copies, waits for them, and re-layouts: 14.9 us -> none  [the longest x1 3.81 us: on_device(): summed = summed.reshape(experts, capacity, width)]
  transfers between devices with their start and end apart: 2 -> 0, of which waited for: 2 -> 0; matrix products, arithmetic and copies ran while one was open for 0% -> 0% of each run, Pallas kernels for 0% -> 0%
where the time goes in v1:
time: 197 us
  Pallas kernels  189 us (96%)
  other arithmetic  5.38 us (3%)
  local copies, waits for them, and re-layouts  2.82 us (1%)
    pallas_call x1, Pallas kernels, on_device(): pl.pallas_call(functools.partial(kernel, E, NX, rows, width), out_shape=j...  189 us

profile of v1, /device:TPU:33, one launch (start us, length us, event | category | flops | bytes accessed | tf_op | source)
XLA Modules:
  0.0 196.8 jit_solution(11538278878401834705)
XLA Ops:
  0.0 1.2 fusion
  1.2 0.8 copy.12
  2.0 0.1 eq.15
  2.1 0.2 convert_reduce_fusion
  2.2 0.1 reduce_sum.22
  2.4 0.1 copy.13
  2.4 0.7 convert_bitcast_fusion
  3.1 1.4 fusion.4.meta
  4.5 1.9 fusion.2.norm
  6.4 188.6 %shard_map.73 = bf16[32,6144]{1,0:T(8,128)(2,1)} custom-call(bf16[32,6144]{1,0:T(8,128)(2,1)} %fusion.2.norm, f32[8,128]{1,0:T(8,128)} %fusion.4.meta, bf16[1,6144,256]{2,1,0:T(8,128)(2,1)} %wg_in.1, bf16[1,6144,256]{2,1,0:T(8,128)(2,1)} %wu_in.1, bf16[1,256,6144]{2,1,0:T(8,128)(2,1)} %wd_in.1), custom_call_target="tpu_custom_call" | custom-call | tf_op jit(solution)/shard_map/pallas_call | solution.py:435
  195.1 1.8 copy.15
  (1 shorter events, 0.0 us)

commit v2 on v1

--- a/solution.py
+++ b/solution.py
@@ -13,7 +13,7 @@
 DMA = pltpu.SemaphoreType.DMA
 
 
-def kernel(E, NX, rows, width, norm, meta, wg_in, wu_in, wd_in, out,
+def kernel(E, NX, rows, width, tokens, ids, scores, gain, wg_in, wu_in, wd_in, out,
            T, M, FS, G, WG, WU, WD, ACC, HID, PB, OPP, RX, R, FR, C, CP, CR, RZ,
            wsem, zs, zr, ps, pr, zms, zmr, pms, pmr, fs, fr, xs, xr, xfs, xfr,
            os_, or_, ms_, mr_, bs, br, cs_, cr_, rs, rr):
@@ -51,19 +51,17 @@
         return 0 if j == 0 else 2 * j - 1 + d
 
     def z_meta(d, j):
-        return rcopy(meta if j == 0 else M.at[idx(d, j), 0], M.at[idx(d, j + 1), 0],
+        return rcopy(M.at[idx(d, j), 0], M.at[idx(d, j + 1), 0],
                      zms.at[d, j], zmr.at[d, j], at_z(sgn[d]))
 
     def p_meta(o):
-        return rcopy(meta if o == 0 else M.at[o, 0], M.at[o, 1], pms.at[o], pmr.at[o], partner)
+        return rcopy(M.at[o, 0], M.at[o, 1], pms.at[o], pmr.at[o], partner)
 
     def z_tok(d, j, f):
-        src = norm.at[:, cols(f)] if j == 0 else T.at[idx(d, j), 0, :, cols(f)]
-        return rcopy(src, T.at[idx(d, j + 1), 0, :, cols(f)], zs.at[d, j, f], zr.at[d, j, f], at_z(sgn[d]))
+        return rcopy(T.at[idx(d, j), 0, :, cols(f)], T.at[idx(d, j + 1), 0, :, cols(f)], zs.at[d, j, f], zr.at[d, j, f], at_z(sgn[d]))
 
     def p_tok(o, f):
-        src = norm.at[:, cols(f)] if o == 0 else T.at[o, 0, :, cols(f)]
-        return rcopy(src, T.at[o, 1, :, cols(f)], ps.at[o, f], pr.at[o, f], partner)
+        return rcopy(T.at[o, 0, :, cols(f)], T.at[o, 1, :, cols(f)], ps.at[o, f], pr.at[o, f], partner)
 
     def far(d, i, f):
         if i == HOP:
@@ -73,36 +71,42 @@
         return rcopy(FS.at[d, i - 1, :, cols(f)], G.at[0, idx(d, HOP + i), :, cols(f)],
                      fs.at[d, i - 1, f], fr.at[d, i - 1, f], at_z(sgn[d] * i))
 
-    groups = [(0, 3)] + [(2 * j - 1, 2 * j + 1) for j in range(2, 2 * HOP - 1)] + [(Z - 3, Z)]
-    NG = len(groups)
+    mid, NB = 2 * HOP + 1, Z
+    items = [(slice(0, 1), slice(0, width))]
+    items += [(slice(2 * j - 1, 2 * j + 1), slice(0, width)) for j in range(1, HOP + 1)]
+    items += [(slice(mid, NB), slice(f * fw, (f + 1) * fw)) for f in range(PARTS)]
+    FAR = HOP + 1
 
     def half(g, side):
-        b0, b1 = groups[g]
-        cut = b0 + 2 if g == 0 else b0 + 1
-        return slice(b0, cut) if side == 0 else slice(cut, b1)
+        b = items[g][0]
+        cut = b.start if g == 0 else (b.start + b.stop + 1) // 2
+        return slice(b.start, cut) if side == 0 else slice(cut, b.stop)
+
+    def sides(g):
+        return [s for s in (0, 1) if half(g, s).stop > half(g, s).start]
 
     def xsend(g, side):
-        b = slice(*groups[g])
-        return rcopy(G.at[0, b], G.at[1 + side, b], xs.at[g, side], xr.at[g, side], side_dev[side])
+        b, k = items[g]
+        return rcopy(G.at[0, b, :, k], G.at[1 + side, b, :, k], xs.at[g, side], xr.at[g, side], side_dev[side])
 
     def xfwd(g, side):
-        b = half(g, side)
-        return rcopy(G.at[1 + side, b], G.at[3, b], xfs.at[g, side], xfr.at[g, side], side_dev[side])
+        b, k = half(g, side), items[g][1]
+        return rcopy(G.at[1 + side, b, :, k], G.at[3, b, :, k], xfs.at[g, side], xfr.at[g, side], side_dev[side])
 
     def opp(g, side):
-        b = half(g, side)
-        return rcopy(PB.at[3, b], OPP.at[b], os_.at[g, side], or_.at[g, side], side_dev[side])
+        b, k = half(g, side), items[g][1]
+        return rcopy(PB.at[3, b, :, k], OPP.at[b, :, k], os_.at[g, side], or_.at[g, side], side_dev[side])
 
     def main(g, side):
-        b = slice(*groups[g])
-        return rcopy(PB.at[2 - side, b], RX.at[side, b], ms_.at[g, side], mr_.at[g, side], side_dev[side])
-
-    def back(d, i):
+        b, k = items[g]
+        return rcopy(PB.at[2 - side, b, :, k], RX.at[side, b, :, k], ms_.at[g, side], mr_.at[g, side], side_dev[side])
+
+    def back(d, i, f):
         if i == HOP:
-            return rcopy(R.at[Z - 1], FR.at[c, i - 1], bs.at[0, i - 1], br.at[0, i - 1],
+            return rcopy(R.at[Z - 1, :, cols(f)], FR.at[c, i - 1, :, cols(f)], bs.at[0, i - 1, f], br.at[0, i - 1, f],
                          {"expert": lax.rem(e - 2 * i * (1 - 2 * c) + 2 * E, E)})
-        return rcopy(R.at[idx(d, HOP + i)], FR.at[d, i - 1], bs.at[d, i - 1], br.at[d, i - 1],
-                     at_z(-sgn[d] * i))
+        return rcopy(R.at[idx(d, HOP + i), :, cols(f)], FR.at[d, i - 1, :, cols(f)],
+                     bs.at[d, i - 1, f], br.at[d, i - 1, f], at_z(-sgn[d] * i))
 
     def p_con(o, f):
         return rcopy(CP.at[o, :, cols(f)], CR.at[o, :, cols(f)], cs_.at[o, f], cr_.at[o, f], partner)
@@ -137,45 +141,65 @@
     def select(lhs, o, f):
         return jnp.dot(lhs, T[o, :, :, cols(f)].reshape(2 * rows, fw), preferred_element_type=F32)
 
-    def ffn_in(b0, b1):
-        n = NX * (b1 - b0) * blk
-        kc = width // 6
-        ACC[:, 0:n] = jnp.zeros((2, n, hid), F32)
-
-        def step(k, carry):
-            ks = pl.ds(pl.multiple_of(k * kc, kc), kc)
-            lhs = G[:, b0:b1, :, ks].reshape(n, kc)
+    kc = fw // 2
+
+    def ffn_in(b, k, fresh=True, done=True):
+        n = NX * (b.stop - b.start) * blk
+        if fresh:
+            ACC[:, 0:n] = jnp.zeros((2, n, hid), F32)
+
+        def step(i, carry):
+            ks = pl.ds(pl.multiple_of(k.start + i * kc, kc), kc)
+            lhs = G[:, b, :, ks].reshape(n, kc)
             ACC[0, 0:n] += jnp.dot(lhs, WG[ks, :], preferred_element_type=F32)
             ACC[1, 0:n] += jnp.dot(lhs, WU[ks, :], preferred_element_type=F32)
             return carry
-        lax.fori_loop(0, 6, step, 0)
-        gate = ACC[0, 0:n]
-        h = gate / (1.0 + jnp.exp(-gate)) * ACC[1, 0:n]
-        HID[:, b0:b1] = h.astype(BF16).reshape(NX, b1 - b0, blk, hid)
+        lax.fori_loop(0, (k.stop - k.start) // kc, step, 0)
+        if done:
+            gate = ACC[0, 0:n]
+            h = gate / (1.0 + jnp.exp(-gate)) * ACC[1, 0:n]
+            HID[:, b] = h.astype(BF16).reshape(NX, b.stop - b.start, blk, hid)
 
     def ffn_out(g):
-        b0, b1 = groups[g]
-        n = NX * (b1 - b0) * blk
-        kc = width // 6
-        lhs = HID[:, b0:b1].reshape(n, hid)
-
-        def step(k, carry):
-            ks = pl.ds(pl.multiple_of(k * kc, kc), kc)
-            PB[:, b0:b1, :, ks] = jnp.dot(lhs, WD[:, ks], preferred_element_type=F32).astype(BF16).reshape(NX, b1 - b0, blk, kc)
+        b, k = items[g]
+        n = NX * (b.stop - b.start) * blk
+        lhs = HID[:, b].reshape(n, hid)
+
+        def step(i, carry):
+            ks = pl.ds(pl.multiple_of(k.start + i * kc, kc), kc)
+            PB[:, b, :, ks] = jnp.dot(lhs, WD[:, ks], preferred_element_type=F32).astype(BF16).reshape(NX, b.stop - b.start, blk, kc)
             return carry
-        lax.fori_loop(0, 6, step, 0)
-
+        lax.fori_loop(0, (k.stop - k.start) // kc, step, 0)
+
+    barrier = pltpu.get_barrier_semaphore()
+    peers = [at_z(s * k) for k in range(1, HOP + 1) for s in sgn] + list(side_dev) + [partner]
+    for dev in peers:
+        pl.semaphore_signal(barrier, inc=1, device_id=dev, device_id_type=MESH)
     weights = [pltpu.make_async_copy(wg_in.at[0], WG, wsem.at[0]),
                pltpu.make_async_copy(wu_in.at[0], WU, wsem.at[1]),
                pltpu.make_async_copy(wd_in.at[0], WD, wsem.at[2])]
     for w in weights:
         w.start()
-    barrier = pltpu.get_barrier_semaphore()
-    peers = [at_z(s * k) for k in range(1, HOP + 1) for s in sgn] + list(side_dev) + [partner]
-    for dev in peers:
-        pl.semaphore_signal(barrier, inc=1, device_id=dev, device_id_type=MESH)
-    T[0, 0] = norm[...]
-    M[0, 0] = meta[...]
+
+    row_t = lax.broadcasted_iota(jnp.int32, (rows, rows), 0)
+    col_t = lax.broadcasted_iota(jnp.int32, (rows, rows), 1)
+    named = [ids[k:k + 1, :].astype(F32) for k in (0, 1)]
+    stood = [jnp.sum(jnp.where(row_t == col_t, r, 0.0), axis=1, keepdims=True) for r in named]
+    M[0, 0] = jnp.zeros((8, 128), F32)
+    for k in (0, 1):
+        ahead = [jnp.where((q == named[k]) & (row_t < col_t), 1.0, 0.0) for q in stood]
+        M[0, 0, k:k + 1, 0:rows] = named[k] * cap + jnp.sum(ahead[0] + ahead[1], axis=0, keepdims=True)
+        M[0, 0, 2 + k:3 + k, 0:rows] = scores[k:k + 1, :]
+    once = M[0, 0]
+    M[0, 0] = jnp.where(lane < 2 * rows, once + pltpu.roll(once, rows, 1), -1.0)
+
+    total = jnp.zeros((rows, 1), F32)
+    for k in range(0, width, kc):
+        t = tokens[:, k:k + kc].astype(F32)
+        total = total + jnp.sum(t * t, axis=1, keepdims=True)
+    scale = lax.rsqrt(total / width + 1e-05)
+    for k in range(0, width, kc):
+        T[0, 0, :, k:k + kc] = (tokens[:, k:k + kc].astype(F32) * scale * gain[:, k:k + kc]).astype(BF16)
     FR[1 - c, HOP - 1] = jnp.zeros((blk, width), BF16)
     pl.semaphore_wait(barrier, len(peers))
 
@@ -216,12 +240,14 @@
     def forward(g):
         for side in (0, 1):
             xsend(g, side).wait_recv()
-            go(xfwd, g, side)
+            if side in sides(g):
+                go(xfwd, g, side)
 
     def gathered(g):
-        for side in (0, 1):
+        for side in sides(g):
             xfwd(g, side).wait_recv()
 
+    spread(0)
     for j in range(1, HOP + 1):
         for d in (0, 1):
             z_meta(d, j - 1).wait_recv()
@@ -265,63 +291,72 @@
                 for d in (0, 1):
                     note(far, d, i)
             note(far, 0, HOP)
-        spread(j - 1)
-        if j > 1:
-            forward(j - 2)
+        spread(j)
+        forward(j - 1)
 
     for w in weights:
         w.wait()
-    gathered(0)
-    gathered(1)
-    ffn_in(0, 5)
-    for i in range(1, HOP):
-        for d in (0, 1):
-            each_part(lambda f: far(d, i, f).wait_recv())
-        if i == HOP - 1:
-            each_part(lambda f: far(0, HOP, f).wait_recv())
-        spread(HOP + i - 1)
-        forward(HOP + i - 2)
-        if i == 2:
-            gathered(2)
-            gathered(3)
-            ffn_in(5, 9)
-    forward(NG - 1)
-    gathered(4)
-    gathered(5)
-    ffn_in(9, 13)
+    full = slice(0, width)
+    for g in range(HOP - 1):
+        gathered(g)
+    ffn_in(slice(0, 2 * HOP - 3), full)
+    for f in range(PARTS):
+        for i in range(1, HOP):
+            for d in (0, 1):
+                far(d, i, f).wait_recv()
+        far(0, HOP, f).wait_recv()
+        spread(FAR + f)
+        forward(FAR + f - 1)
+        if f == PARTS - 2:
+            gathered(HOP - 1)
+            gathered(HOP)
+            ffn_in(slice(2 * HOP - 3, mid), full)
+    for g in range(HOP, -1, -1):
+        ffn_out(g)
+    far_blocks = slice(mid, NB)
+    for f in range(PARTS):
+        if f == PARTS - 1:
+            forward(FAR + f)
+        gathered(FAR + f)
+        ffn_in(far_blocks, items[FAR + f][1], f == 0, f == PARTS - 1)
 
     def begin(g):
-        ffn_out(g)
-        go(opp, g, 0)
-        go(opp, g, 1)
+        if g >= FAR:
+            ffn_out(g)
+        for side in sides(g):
+            go(opp, g, side)
 
     def middle(g):
+        k = items[g][1]
         for side in (0, 1):
-            b = half(g, side)
-            n = b.stop - b.start
-            opp(g, side).wait_recv()
-
-            def add(f):
-                PB[2 - side, b, :, cols(f)] = (PB[2 - side, b, :, cols(f)].astype(F32) + OPP[b, :, cols(f)].astype(F32)).astype(BF16)
-            each_part(add)
+            if side in sides(g):
+                b = half(g, side)
+                opp(g, side).wait_recv()
+
+                def add(i, carry):
+                    ks = pl.ds(pl.multiple_of(k.start + i * kc, kc), kc)
+                    PB[2 - side, b, :, ks] = (PB[2 - side, b, :, ks].astype(F32) + OPP[b, :, ks].astype(F32)).astype(BF16)
+                    return carry
+                lax.fori_loop(0, (k.stop - k.start) // kc, add, 0)
             go(main, g, side)
 
     def finish(g):
-        b = slice(*groups[g])
+        b, k = items[g]
         for side in (0, 1):
             main(g, side).wait_recv()
 
-        def add(f):
-            R[b, :, cols(f)] = (PB[0, b, :, cols(f)].astype(F32) + RX[0, b, :, cols(f)].astype(F32)
-                                + RX[1, b, :, cols(f)].astype(F32)).astype(BF16)
-        each_part(add)
-
-    def far_back(g):
-        i = g - HOP + 1
-        for d in (0, 1):
-            go(back, d, i)
-        if g == NG - 1:
-            go(back, 0, HOP)
+        def add(i, carry):
+            ks = pl.ds(pl.multiple_of(k.start + i * kc, kc), kc)
+            R[b, :, ks] = (PB[0, b, :, ks].astype(F32) + RX[0, b, :, ks].astype(F32)
+                           + RX[1, b, :, ks].astype(F32)).astype(BF16)
+            return carry
+        lax.fori_loop(0, (k.stop - k.start) // kc, add, 0)
+        if g >= FAR:
+            f = g - FAR
+            go(back, 0, HOP, f)
+            for i in range(HOP - 1, 0, -1):
+                for d in (0, 1):
+                    go(back, d, i, f)
 
     def weigh(lhs, rhs):
         return lax.dot_general(lhs, rhs, (((0,), (0,)), ((), ())), preferred_element_type=F32)
@@ -333,14 +368,14 @@
             w_far = None
             if j == HOP:
                 w_far = beyond(o, d, True)
-                for i in range(1, HOP):
-                    back(d, i).wait_recv()
-                if d == 0:
-                    back(0, HOP).wait_recv()
 
             def step(f):
                 u = weigh(w_own, R[o, :, cols(f)])
                 if j == HOP:
+                    for i in range(1, HOP):
+                        back(d, i, f).wait_recv()
+                    if d == 0:
+                        back(0, HOP, f).wait_recv()
                     u = u + weigh(w_far, FR[d, :, :, cols(f)].reshape(HOP * blk, fw))
                 C[o, :, cols(f)] = u[:rows].astype(BF16)
                 CP[o, :, cols(f)] = u[rows:].astype(BF16)
@@ -363,39 +398,26 @@
         note(ring, 0, j)
         note(ring, 1, j)
 
-    begin(4)
-    begin(5)
-    gathered(6)
-    ffn_in(13, 16)
-    begin(6)
-    middle(4)
-    middle(5)
-    begin(3)
-    middle(6)
-    finish(4)
-    far_back(4)
-    finish(5)
-    far_back(5)
-    middle(3)
-    finish(6)
-    far_back(6)
-    begin(2)
-    finish(3)
-    middle(2)
-    begin(1)
-    give(4)
-    pass_on(4)
-    finish(2)
-    give(3)
-    middle(1)
-    begin(0)
-    pass_on(3)
+    far_items = list(range(FAR, FAR + PARTS))
+    order = far_items + list(range(HOP, -1, -1))
+    begin(order[0])
+    for n, g in enumerate(order):
+        if n + 1 < len(order):
+            begin(order[n + 1])
+        middle(g)
+        if n >= 2:
+            h = order[n - 2]
+            finish(h)
+            if h < FAR:
+                give(h)
+            if h == HOP:
+                pass_on(h)
+            if h + 1 < HOP and h < FAR:
+                pass_on(h + 1)
     finish(1)
-    give(2)
-    middle(0)
+    give(1)
     pass_on(2)
     finish(0)
-    give(1)
     give(0)
     pass_on(1)
 
@@ -419,23 +441,12 @@
     E, NX = lax.axis_size("expert"), lax.axis_size("tensor")
     cap = 4 * rows // E
     Z, HOP, blk, hid = E // 2, E // 8, 2 * cap, w_gate.shape[2]
-    values = tokens.astype(F32)
-    scale = lax.rsqrt(jnp.mean(values * values, axis=-1, keepdims=True) + 1e-05)
-    normed = (values * scale * norm_gain).astype(BF16)
-    flat = expert_ids.reshape(-1)
-    n = flat.shape[0]
-    order = jnp.arange(n, dtype=jnp.int32)
-    same = (flat[:, None] == flat[None, :]) & (order[None, :] < order[:, None])
-    target = (flat * cap + jnp.sum(same.astype(jnp.int32), axis=1)).reshape(rows, -1).astype(F32)
-    info = jnp.concatenate([target.T, gate_scores.T], axis=0)
-    info = jnp.concatenate([info, info], axis=1)
-    meta = jnp.full((8, 128), -1.0, F32).at[:4, :2 * rows].set(info)
-    NG, NO = 2 * HOP - 1, 2 * HOP + 1
+    NG, NO = HOP + 1 + PARTS, 2 * HOP + 1
     v = lambda *s: pltpu.VMEM(s, BF16)
     return pl.pallas_call(
         functools.partial(kernel, E, NX, rows, width),
         out_shape=jax.ShapeDtypeStruct((rows, width), BF16),
-        in_specs=[pl.BlockSpec(memory_space=pltpu.VMEM)] * 2 + [pl.BlockSpec(memory_space=pl.ANY)] * 3,
+        in_specs=[pl.BlockSpec(memory_space=pltpu.VMEM)] * 4 + [pl.BlockSpec(memory_space=pl.ANY)] * 3,
         out_specs=pl.BlockSpec(memory_space=pltpu.VMEM),
         scratch_shapes=[
             v(NO, 2, rows, width),
@@ -443,7 +454,7 @@
             v(2, HOP, blk, width),
             v(NX, Z, blk, width),
             v(width, hid), v(width, hid), v(hid, width),
-            pltpu.VMEM((2, NX * 5 * blk, hid), F32),
+            pltpu.VMEM((2, NX * (Z - NO) * blk, hid), F32),
             v(NX, Z, blk, hid),
             v(NX, Z, blk, width),
             v(Z, blk, width),
@@ -458,12 +469,12 @@
             DMA((2, HOP, PARTS)), DMA((2, HOP, PARTS)),
             DMA((NG, 2)), DMA((NG, 2)), DMA((NG, 2)), DMA((NG, 2)),
             DMA((NG, 2)), DMA((NG, 2)), DMA((NG, 2)), DMA((NG, 2)),
-            DMA((2, HOP)), DMA((2, HOP)),
+            DMA((2, HOP, PARTS)), DMA((2, HOP, PARTS)),
             DMA((NO, PARTS)), DMA((NO, PARTS)),
             DMA((2, HOP, PARTS)), DMA((2, HOP, PARTS)),
         ],
         compiler_params=pltpu.CompilerParams(collective_id=0, has_side_effects=True, vmem_limit_bytes=63 * 1024 * 1024),
-    )(normed, meta, w_gate, w_up, w_down)
+    )(tokens, expert_ids.T, gate_scores.T, norm_gain.reshape(1, width), w_gate, w_up, w_down)
 
 
 def solution(mesh):

time: 197 us -> 188 us (0.954)
  other arithmetic: 5.38 us -> 0 us
  Pallas kernels: 189 us -> 186 us
    pallas_call x1, Pallas kernels: 189 us -> 186 us  [on_device(): pl.pallas_call(functools.partial(kernel, E, NX, rows, width), out_shape=j...]
where the time goes in v2:
time: 188 us
  Pallas kernels  186 us (99%)
    pallas_call x1, Pallas kernels, on_device(): pl.pallas_call(functools.partial(kernel, E, NX, rows, width), out_shape=j...  186 us

profile of v2, /device:TPU:33, one launch (start us, length us, event | category | flops | bytes accessed | tf_op | source)
XLA Modules:
  0.0 187.8 jit_solution(11907263366516666746)
XLA Ops:
  0.0 186.0 %shard_map.73 = bf16[32,6144]{1,0:T(8,128)(2,1)} custom-call(bf16[32,6144]{1,0:T(8,128)(2,1)} %tokens.1, s32[2,32]{1,0:T(2,128)} %bitcast.4, f32[2,32]{1,0:T(2,128)} %bitcast.5, f32[1,6144]{1,0:T(1,128)} %bitcast.3, bf16[1,6144,256]{2,1,0:T(8,128)(2,1)} %wg_in.1, bf16[1,6144,256]{2,1,0:T(8,128)(2,1)} %wu_in.1, bf16[1,256,6144]{2,1,0:T(8,128)(2,1)} %wd_in.1), custom_call_target="tpu_custom_call" | custom-call | tf_op jit(solution)/shard_map/pallas_call | solution.py:446
  186.0 1.8 copy.9

commit v3 on v2

--- a/solution.py
+++ b/solution.py
@@ -9,7 +9,8 @@
 
 MESH = pl.DeviceIdType.MESH
 F32, BF16 = jnp.float32, jnp.bfloat16
-PARTS = 3
+PARTS = 6
+ROUNDS = 2
 DMA = pltpu.SemaphoreType.DMA
 
 
@@ -41,11 +42,14 @@
         return pltpu.make_async_remote_copy(src_ref=src, dst_ref=dst, send_sem=s, recv_sem=r,
                                             device_id=dev, device_id_type=MESH)
 
-    def each_part(body):
+    PR = PARTS // ROUNDS
+    wr = width // ROUNDS
+
+    def each_part(h, body):
         def step(f, carry):
             body(f)
             return carry
-        lax.fori_loop(0, PARTS, step, 0)
+        lax.fori_loop(h * PR, (h + 1) * PR, step, 0)
 
     def idx(d, j):
         return 0 if j == 0 else 2 * j - 1 + d
@@ -72,14 +76,19 @@
                      fs.at[d, i - 1, f], fr.at[d, i - 1, f], at_z(sgn[d] * i))
 
     mid, NB = 2 * HOP + 1, Z
-    items = [(slice(0, 1), slice(0, width))]
-    items += [(slice(2 * j - 1, 2 * j + 1), slice(0, width)) for j in range(1, HOP + 1)]
+    items = []
+    for h in range(ROUNDS):
+        items.append((slice(0, 1), slice(h * wr, (h + 1) * wr)))
+        items += [(slice(2 * j - 1, 2 * j + 1), slice(h * wr, (h + 1) * wr)) for j in range(1, HOP + 1)]
+    FAR = len(items)
     items += [(slice(mid, NB), slice(f * fw, (f + 1) * fw)) for f in range(PARTS)]
-    FAR = HOP + 1
+
+    def near(h, j):
+        return h * (HOP + 1) + j
 
     def half(g, side):
         b = items[g][0]
-        cut = b.start if g == 0 else (b.start + b.stop + 1) // 2
+        cut = b.start if b.start == 0 else (b.start + b.stop + 1) // 2
         return slice(b.start, cut) if side == 0 else slice(cut, b.stop)
 
     def sides(g):
@@ -141,24 +150,23 @@
     def select(lhs, o, f):
         return jnp.dot(lhs, T[o, :, :, cols(f)].reshape(2 * rows, fw), preferred_element_type=F32)
 
-    kc = fw // 2
-
-    def ffn_in(b, k, fresh=True, done=True):
+    kc = fw
+
+    def ffn_in(b, k):
         n = NX * (b.stop - b.start) * blk
-        if fresh:
-            ACC[:, 0:n] = jnp.zeros((2, n, hid), F32)
 
         def step(i, carry):
             ks = pl.ds(pl.multiple_of(k.start + i * kc, kc), kc)
             lhs = G[:, b, :, ks].reshape(n, kc)
-            ACC[0, 0:n] += jnp.dot(lhs, WG[ks, :], preferred_element_type=F32)
-            ACC[1, 0:n] += jnp.dot(lhs, WU[ks, :], preferred_element_type=F32)
+            for m, W in ((0, WG), (1, WU)):
+                got = jnp.dot(lhs, W[ks, :], preferred_element_type=F32)
+                ACC[m, :, b] += got.reshape(NX, b.stop - b.start, blk, hid)
             return carry
         lax.fori_loop(0, (k.stop - k.start) // kc, step, 0)
-        if done:
-            gate = ACC[0, 0:n]
-            h = gate / (1.0 + jnp.exp(-gate)) * ACC[1, 0:n]
-            HID[:, b] = h.astype(BF16).reshape(NX, b.stop - b.start, blk, hid)
+
+    def ffn_mid(b):
+        gate = ACC[0, :, b]
+        HID[:, b] = (gate / (1.0 + jnp.exp(-gate)) * ACC[1, :, b]).astype(BF16)
 
     def ffn_out(g):
         b, k = items[g]
@@ -200,6 +208,7 @@
     scale = lax.rsqrt(total / width + 1e-05)
     for k in range(0, width, kc):
         T[0, 0, :, k:k + kc] = (tokens[:, k:k + kc].astype(F32) * scale * gain[:, k:k + kc]).astype(BF16)
+    ACC[...] = jnp.zeros_like(ACC)
     FR[1 - c, HOP - 1] = jnp.zeros((blk, width), BF16)
     pl.semaphore_wait(barrier, len(peers))
 
@@ -207,31 +216,24 @@
 
     def go(make, *a):
         make(*a).start()
-        sent.append((make, a, False))
-
-    def note(make, *a):
-        sent.append((make, a, True))
+        sent.append((make, a, None))
+
+    def note(h, make, *a):
+        sent.append((make, a, h))
 
     for d in (0, 1):
         go(z_meta, d, 0)
     go(p_meta, 0)
 
-    def first(f):
-        p_tok(0, f).start()
-        z_tok(0, 0, f).start()
-        z_tok(1, 0, f).start()
-    each_part(first)
-    note(p_tok, 0)
-    note(z_tok, 0, 0)
-    note(z_tok, 1, 0)
-
-    p_meta(0).wait_recv()
-    lhs0 = own(0, False)
-
-    def sel0(f):
-        p_tok(0, f).wait_recv()
-        G[0, 0, :, cols(f)] = select(lhs0, 0, f).astype(BF16)
-    each_part(sel0)
+    def launch(h):
+        def first(f):
+            p_tok(0, f).start()
+            z_tok(0, 0, f).start()
+            z_tok(1, 0, f).start()
+        each_part(h, first)
+        note(h, p_tok, 0)
+        note(h, z_tok, 0, 0)
+        note(h, z_tok, 1, 0)
 
     def spread(g):
         go(xsend, g, 0)
@@ -247,27 +249,36 @@
         for side in sides(g):
             xfwd(g, side).wait_recv()
 
-    spread(0)
-    for j in range(1, HOP + 1):
+    def own_chip(h):
+        lhs = own(0, False)
+
+        def sel(f):
+            p_tok(0, f).wait_recv()
+            G[0, 0, :, cols(f)] = select(lhs, 0, f).astype(BF16)
+        each_part(h, sel)
+        spread(near(h, 0))
+
+    def meta_hop(j):
         for d in (0, 1):
             z_meta(d, j - 1).wait_recv()
             if j < HOP:
                 go(z_meta, d, j)
             go(p_meta, idx(d, j))
 
-        def hop(f):
+    def hop(h, j):
+        def step(f):
             for d in (0, 1):
                 z_tok(d, j - 1, f).wait_recv()
                 if j < HOP:
                     z_tok(d, j, f).start()
                 p_tok(idx(d, j), f).start()
-        each_part(hop)
+        each_part(h, step)
         for d in (0, 1):
             if j < HOP:
-                note(z_tok, d, j)
-            note(p_tok, idx(d, j))
-        for d in (0, 1):
-            p_meta(idx(d, j)).wait_recv()
+                note(h, z_tok, d, j)
+            note(h, p_tok, idx(d, j))
+
+    def choose(h, j):
         lhs = [own(idx(d, j), False) for d in (0, 1)]
         if j == HOP:
             lhs = [jnp.concatenate([lhs[d], beyond(idx(d, j), d, False)], axis=0) for d in (0, 1)]
@@ -285,43 +296,78 @@
                     for d in (0, 1):
                         far(d, i, f).start()
                 far(0, HOP, f).start()
-        each_part(sel)
+        each_part(h, sel)
         if j == HOP:
             for i in range(1, HOP):
                 for d in (0, 1):
-                    note(far, d, i)
-            note(far, 0, HOP)
-        spread(j)
-        forward(j - 1)
-
-    for w in weights:
-        w.wait()
-    full = slice(0, width)
-    for g in range(HOP - 1):
-        gathered(g)
-    ffn_in(slice(0, 2 * HOP - 3), full)
-    for f in range(PARTS):
+                    note(h, far, d, i)
+            note(h, far, 0, HOP)
+        spread(near(h, j))
+
+    def far_in(f):
         for i in range(1, HOP):
             for d in (0, 1):
                 far(d, i, f).wait_recv()
         far(0, HOP, f).wait_recv()
         spread(FAR + f)
-        forward(FAR + f - 1)
-        if f == PARTS - 2:
-            gathered(HOP - 1)
-            gathered(HOP)
-            ffn_in(slice(2 * HOP - 3, mid), full)
-    for g in range(HOP, -1, -1):
-        ffn_out(g)
-    far_blocks = slice(mid, NB)
-    for f in range(PARTS):
-        if f == PARTS - 1:
-            forward(FAR + f)
+
+    nears, fars = slice(0, mid), slice(mid, NB)
+
+    launch(0)
+    p_meta(0).wait_recv()
+    before = None
+    for h in range(ROUNDS):
+        own_chip(h)
+        if before is not None:
+            forward(before)
+        before = near(h, 0)
+        for j in range(1, HOP + 1):
+            if h == 0:
+                meta_hop(j)
+            hop(h, j)
+            if j == HOP and h + 1 < ROUNDS:
+                launch(h + 1)
+            if h == 0:
+                for d in (0, 1):
+                    p_meta(idx(d, j)).wait_recv()
+            choose(h, j)
+            forward(before)
+            before = near(h, j)
+            if h > 0 and j == 1:
+                for f in range((h - 1) * PR, h * PR):
+                    far_in(f)
+                    forward(before)
+                    before = FAR + f
+            if h > 0 and j == HOP - 1:
+                if h == 1:
+                    for w in weights:
+                        w.wait()
+                for jj in range(HOP + 1):
+                    gathered(near(h - 1, jj))
+                ffn_in(nears, slice((h - 1) * wr, h * wr))
+            if h > 0 and j == HOP:
+                for f in range((h - 1) * PR, h * PR):
+                    gathered(FAR + f)
+                ffn_in(fars, slice((h - 1) * wr, h * wr))
+    h = ROUNDS - 1
+    for f in range(h * PR, PARTS):
+        far_in(f)
+        forward(before)
+        before = FAR + f
+    for j in range(HOP + 1):
+        gathered(near(h, j))
+    ffn_in(nears, slice(h * wr, width))
+    ffn_mid(nears)
+    forward(before)
+    for j in range(HOP, -1, -1):
+        ffn_out(near(0, j))
+    for f in range(h * PR, PARTS):
         gathered(FAR + f)
-        ffn_in(far_blocks, items[FAR + f][1], f == 0, f == PARTS - 1)
+        ffn_in(fars, items[FAR + f][1])
+    ffn_mid(fars)
 
     def begin(g):
-        if g >= FAR:
+        if g > HOP:
             ffn_out(g)
         for side in sides(g):
             go(opp, g, side)
@@ -361,13 +407,11 @@
     def weigh(lhs, rhs):
         return lax.dot_general(lhs, rhs, (((0,), (0,)), ((), ())), preferred_element_type=F32)
 
-    def give(j):
+    def give(h, j):
         for d in ((0, 1) if j > 0 else (0,)):
             o = idx(d, j)
             w_own = own(o, True)
-            w_far = None
-            if j == HOP:
-                w_far = beyond(o, d, True)
+            w_far = beyond(o, d, True) if j == HOP else None
 
             def step(f):
                 u = weigh(w_own, R[o, :, cols(f)])
@@ -380,10 +424,10 @@
                 C[o, :, cols(f)] = u[:rows].astype(BF16)
                 CP[o, :, cols(f)] = u[rows:].astype(BF16)
                 p_con(o, f).start()
-            each_part(step)
-            note(p_con, o)
-
-    def pass_on(j):
+            each_part(h, step)
+            note(h, p_con, o)
+
+    def pass_on(h, j):
         def step(f):
             for d in (0, 1):
                 o = idx(d, j)
@@ -394,46 +438,53 @@
                     v = v + RZ[d, j, :, cols(f)].astype(F32)
                 C[o, :, cols(f)] = v.astype(BF16)
                 ring(d, j, f).start()
-        each_part(step)
-        note(ring, 0, j)
-        note(ring, 1, j)
-
-    far_items = list(range(FAR, FAR + PARTS))
-    order = far_items + list(range(HOP, -1, -1))
-    begin(order[0])
-    for n, g in enumerate(order):
-        if n + 1 < len(order):
-            begin(order[n + 1])
-        middle(g)
-        if n >= 2:
-            h = order[n - 2]
-            finish(h)
-            if h < FAR:
-                give(h)
-            if h == HOP:
-                pass_on(h)
-            if h + 1 < HOP and h < FAR:
-                pass_on(h + 1)
-    finish(1)
-    give(1)
-    pass_on(2)
-    finish(0)
-    give(0)
-    pass_on(1)
-
-    def last(f):
-        p_con(0, f).wait_recv()
-        ring(0, 1, f).wait_recv()
-        ring(1, 1, f).wait_recv()
-        out[:, cols(f)] = (C[0, :, cols(f)].astype(F32) + CR[0, :, cols(f)].astype(F32)
-                           + RZ[0, 0, :, cols(f)].astype(F32) + RZ[1, 0, :, cols(f)].astype(F32)).astype(BF16)
-    each_part(last)
-
-    for make, a, looped in sent:
-        if looped:
-            each_part(lambda f: make(*a, f).wait_send())
+        each_part(h, step)
+        note(h, ring, 0, j)
+        note(h, ring, 1, j)
+
+    def last(h):
+        def step(f):
+            p_con(0, f).wait_recv()
+            ring(0, 1, f).wait_recv()
+            ring(1, 1, f).wait_recv()
+            out[:, cols(f)] = (C[0, :, cols(f)].astype(F32) + CR[0, :, cols(f)].astype(F32)
+                               + RZ[0, 0, :, cols(f)].astype(F32) + RZ[1, 0, :, cols(f)].astype(F32)).astype(BF16)
+        each_part(h, step)
+
+    order = []
+    for h in range(ROUNDS):
+        order += [(FAR + f, h, None) for f in range(h * PR, (h + 1) * PR)]
+        order += [(near(h, j), h, j) for j in range(HOP, -1, -1)]
+    lag = 2
+    todo = {}
+    for n, (g, h, j) in enumerate(order):
+        if j == HOP:
+            for k in range(HOP, -1, -1):
+                todo.setdefault(n + lag * (HOP - k), []).append((h, k))
+    begin(order[0][0])
+    begin(order[1][0])
+    steps = max(len(order) + 2, max(todo) + 3)
+    for n in range(steps):
+        if n + 2 < len(order):
+            begin(order[n + 2][0])
+        if n < len(order):
+            middle(order[n][0])
+        if 0 <= n - 2 < len(order):
+            g, h, j = order[n - 2]
+            finish(g)
+            if j is not None:
+                give(h, j)
+        for h, k in todo.get(n - 2, ()):
+            if k > 0:
+                pass_on(h, k)
+            else:
+                last(h)
+
+    for make, a, h in sent:
+        if h is None:
+            make(*a).wait_send()
         else:
-            make(*a).wait_send()
+            each_part(h, lambda f: make(*a, f).wait_send())
 
 
 def on_device(tokens, expert_ids, gate_scores, norm_gain, w_gate, w_up, w_down):
@@ -441,7 +492,7 @@
     E, NX = lax.axis_size("expert"), lax.axis_size("tensor")
     cap = 4 * rows // E
     Z, HOP, blk, hid = E // 2, E // 8, 2 * cap, w_gate.shape[2]
-    NG, NO = HOP + 1 + PARTS, 2 * HOP + 1
+    NG, NO = ROUNDS * (HOP + 1) + PARTS, 2 * HOP + 1
     v = lambda *s: pltpu.VMEM(s, BF16)
     return pl.pallas_call(
         functools.partial(kernel, E, NX, rows, width),
@@ -454,7 +505,7 @@
             v(2, HOP, blk, width),
             v(NX, Z, blk, width),
             v(width, hid), v(width, hid), v(hid, width),
-            pltpu.VMEM((2, NX * (Z - NO) * blk, hid), F32),
+            pltpu.VMEM((2, NX, Z, blk, hid), F32),
             v(NX, Z, blk, hid),
             v(NX, Z, blk, width),
             v(Z, blk, width),

time: 188 us -> 193 us (1.027)
  Pallas kernels: 186 us -> 190 us
    pallas_call x1, Pallas kernels: 186 us -> 190 us  [on_device(): pl.pallas_call(functools.partial(kernel, E, NX, rows, width), out_shape=j...]
where the time goes in v3:
time: 193 us; the launch traced here: 192 us
  Pallas kernels  190 us (98%)
    pallas_call x1, Pallas kernels, on_device(): pl.pallas_call(functools.partial(kernel, E, NX, rows, width), out_shape=j...  190 us

profile of v3, /device:TPU:33, one launch (start us, length us, event | category | flops | bytes accessed | tf_op | source)
XLA Modules:
  0.0 192.0 jit_solution(12340527604601819172)
XLA Ops:
  0.0 190.2 %shard_map.73 = bf16[32,6144]{1,0:T(8,128)(2,1)} custom-call(bf16[32,6144]{1,0:T(8,128)(2,1)} %tokens.1, s32[2,32]{1,0:T(2,128)} %bitcast.4, f32[2,32]{1,0:T(2,128)} %bitcast.5, f32[1,6144]{1,0:T(1,128)} %bitcast.3, bf16[1,6144,256]{2,1,0:T(8,128)(2,1)} %wg_in.1, bf16[1,6144,256]{2,1,0:T(8,128)(2,1)} %wu_in.1, bf16[1,256,6144]{2,1,0:T(8,128)(2,1)} %wd_in.1), custom_call_target="tpu_custom_call" | custom-call | tf_op jit(solution)/shard_map/pallas_call | solution.py:497
  190.2 1.8 copy.9

commit v4 on v0

v4 whole, which is shorter than its diff:
```python
import functools

import jax
import jax.numpy as jnp
from jax import lax
from jax.experimental import pallas as pl
from jax.experimental.pallas import tpu as pltpu
from jax.sharding import PartitionSpec as P

MESH = pl.DeviceIdType.MESH
F32, BF16 = jnp.float32, jnp.bfloat16
PARTS = 4
DMA = pltpu.SemaphoreType.DMA
ORDER = [
    ("L", 0), ("L", 1), ("S", 0, 0), ("L", 2), ("S", 0, 1), ("S", 0, 2), ("L", 3), ("H", 1, 0), ("S", 0, 3),
    ("S", 1, 0), ("X", 0, 0), ("H", 1, 1), ("S", 1, 1), ("X", 0, 1), ("H", 1, 2), ("XF", 0, 0), ("S", 1, 2),
    ("X", 0, 2), ("H", 1, 3), ("XF", 0, 1), ("S", 1, 3), ("X", 0, 3), ("H", 2, 0), ("S", 2, 0), ("XF", 0, 2),
    ("H", 2, 1), ("S", 2, 1), ("XF", 0, 3), ("H", 2, 2), ("S", 2, 2), ("H", 2, 3), ("S", 2, 3), ("H", 3, 0),
    ("S", 3, 0), ("X", 1, 0), ("H", 3, 1), ("S", 3, 1), ("X", 1, 1), ("H", 3, 2), ("S", 3, 2), ("X", 1, 2),
    ("XF", 1, 0), ("H", 3, 3), ("S", 3, 3), ("X", 1, 3), ("XF", 1, 1), ("H", 4, 0), ("S", 4, 0), ("X", 2, 0),
    ("XF", 1, 2), ("H", 4, 1), ("S", 4, 1), ("X", 2, 1), ("H", 4, 2), ("XF", 1, 3), ("S", 4, 2), ("X", 2, 2),
    ("H", 4, 3), ("XF", 2, 0), ("S", 4, 3), ("X", 2, 3), ("XF", 2, 1), ("XF", 2, 2), ("FI", 0, 0), ("X", 3, 0),
    ("XF", 2, 3), ("FI", 0, 1), ("FI", 0, 2), ("X", 3, 1), ("XF", 3, 0), ("FI", 0, 3), ("FM", 0), ("FO", 0, 0),
    ("FO", 0, 1), ("X", 3, 2), ("FO", 0, 2), ("FO", 0, 3), ("XF", 3, 1), ("FI", 1, 0), ("X", 3, 3), ("XF", 3, 2),
    ("FI", 1, 1), ("O", 2, 0), ("O", 1, 0), ("XF", 3, 3), ("FI", 1, 2), ("O", 0, 0), ("M", 2, 0), ("M", 1, 0),
    ("FI", 1, 3), ("FM", 1), ("M", 0, 0), ("FO", 1, 0), ("FO", 1, 1), ("N", 2, 0), ("FO", 1, 2), ("FO", 1, 3),
    ("O", 3, 0), ("N", 1, 0), ("G", 3, 0), ("G", 2, 0), ("O", 3, 1), ("N", 0, 0), ("G", 1, 0), ("G", 0, 0),
    ("O", 3, 2), ("M", 3, 0), ("M", 3, 1), ("M", 3, 2), ("N", 3, 0), ("N", 3, 1), ("O", 2, 1), ("O", 1, 1),
    ("O", 0, 1), ("O", 3, 3), ("G", 4, 0), ("N", 3, 2), ("M", 2, 1), ("P", 4, 0), ("M", 1, 1), ("M", 0, 1),
    ("M", 3, 3), ("N", 2, 1), ("G", 4, 1), ("P", 4, 1), ("N", 1, 1), ("G", 3, 1), ("G", 2, 1), ("N", 0, 1),
    ("G", 1, 1), ("G", 0, 1), ("O", 2, 2), ("P", 3, 0), ("O", 1, 2), ("O", 0, 2), ("O", 2, 3), ("P", 3, 1),
    ("O", 1, 3), ("N", 3, 3), ("M", 2, 2), ("M", 1, 2), ("P", 2, 0), ("M", 0, 2), ("M", 2, 3), ("P", 2, 1),
    ("M", 1, 3), ("N", 2, 2), ("G", 4, 2), ("P", 4, 2), ("N", 1, 2), ("G", 3, 2), ("G", 2, 2), ("O", 0, 3),
    ("N", 0, 2), ("G", 1, 2), ("G", 0, 2), ("N", 2, 3), ("G", 4, 3), ("P", 1, 0), ("P", 4, 3), ("N", 1, 3),
    ("G", 3, 3), ("P", 1, 1), ("G", 2, 3), ("M", 0, 3), ("P", 3, 2), ("E", 0), ("N", 0, 3), ("G", 1, 3), ("G", 0, 3),
    ("P", 3, 3), ("E", 1), ("P", 2, 2), ("P", 2, 3), ("P", 1, 2), ("P", 1, 3), ("E", 2), ("E", 3),
]


def kernel(E, NX, rows, width, tokens, ids, scores, gain, wg_in, wu_in, wd_in, out,
           T, M, FS, G, WG, WU, WD, ACC, HID, PB, OPP, RX, R, FR, C, CP, CR, RZ,
           wsem, zs, zr, ps, pr, zms, zmr, pms, pmr, fs, fr, xs, xr, xfs, xfr,
           os_, or_, ms_, mr_, bs, br, cs_, cr_, rs, rr):
    Z = E // 2
    HOP = Z // 4
    cap = 4 * rows // E
    blk = 2 * cap
    fw = width // PARTS
    hid = WG.shape[1]
    e = lax.axis_index("expert")
    x = lax.axis_index("tensor")
    c = lax.rem(e, 2)
    sgn = (1, -1)

    def at_z(k):
        return {"expert": lax.rem(e + 2 * k + 2 * E, E)}

    partner = {"expert": e + 1 - 2 * c}
    side_dev = ({"tensor": lax.rem(x + 1, NX)}, {"tensor": lax.rem(x + NX - 1, NX)})

    def cols(f):
        return slice(f * fw, (f + 1) * fw)

    def rcopy(src, dst, s, r, dev):
        return pltpu.make_async_remote_copy(src_ref=src, dst_ref=dst, send_sem=s, recv_sem=r,
                                            device_id=dev, device_id_type=MESH)

    def idx(d, j):
        return 0 if j == 0 else 2 * j - 1 + d

    def z_meta(d, j):
        return rcopy(M.at[idx(d, j), 0], M.at[idx(d, j + 1), 0],
                     zms.at[d, j], zmr.at[d, j], at_z(sgn[d]))

    def p_meta(o):
        return rcopy(M.at[o, 0], M.at[o, 1], pms.at[o], pmr.at[o], partner)

    def z_tok(d, j, f):
        return rcopy(T.at[idx(d, j), 0, :, cols(f)], T.at[idx(d, j + 1), 0, :, cols(f)], zs.at[d, j, f], zr.at[d, j, f], at_z(sgn[d]))

    def p_tok(o, f):
        return rcopy(T.at[o, 0, :, cols(f)], T.at[o, 1, :, cols(f)], ps.at[o, f], pr.at[o, f], partner)

    def far(d, i, f):
        if i == HOP:
            return rcopy(FS.at[c, i - 1, :, cols(f)], G.at[0, Z - 1, :, cols(f)],
                         fs.at[0, i - 1, f], fr.at[0, i - 1, f],
                         {"expert": lax.rem(e + 2 * i * (1 - 2 * c) + 2 * E, E)})
        return rcopy(FS.at[d, i - 1, :, cols(f)], G.at[0, idx(d, HOP + i), :, cols(f)],
                     fs.at[d, i - 1, f], fr.at[d, i - 1, f], at_z(sgn[d] * i))

    mid, NB = 2 * HOP + 1, Z
    groups = [(0, 3), (3, 2 * HOP - 1), (2 * HOP - 1, mid), (mid, NB)]
    FARG = len(groups) - 1
    nears, fars = slice(0, mid), slice(mid, NB)

    def half(g, side):
        b0, b1 = groups[g]
        cut = (b0 + b1 + (g == FARG)) // 2
        return slice(b0, cut) if side == 0 else slice(cut, b1)

    def xsend(g, f, side):
        b, k, n = slice(*groups[g]), cols(f), g * PARTS + f
        return rcopy(G.at[0, b, :, k], G.at[1 + side, b, :, k], xs.at[n, side], xr.at[n, side], side_dev[side])

    def xfwd(g, f, side):
        b, k, n = half(g, side), cols(f), g * PARTS + f
        return rcopy(G.at[1 + side, b, :, k], G.at[3, b, :, k], xfs.at[n, side], xfr.at[n, side], side_dev[side])

    def opp(g, f, side):
        b, k, n = half(g, side), cols(f), g * PARTS + f
        return rcopy(PB.at[3, b, :, k], OPP.at[b, :, k], os_.at[n, side], or_.at[n, side], side_dev[side])

    def main(g, f, side):
        b, k, n = slice(*groups[g]), cols(f), g * PARTS + f
        return rcopy(PB.at[2 - side, b, :, k], RX.at[side, b, :, k], ms_.at[n, side], mr_.at[n, side], side_dev[side])

    def back(d, i, f):
        if i == HOP:
            return rcopy(R.at[Z - 1, :, cols(f)], FR.at[c, i - 1, :, cols(f)], bs.at[0, i - 1, f], br.at[0, i - 1, f],
                         {"expert": lax.rem(e - 2 * i * (1 - 2 * c) + 2 * E, E)})
        return rcopy(R.at[idx(d, HOP + i), :, cols(f)], FR.at[d, i - 1, :, cols(f)],
                     bs.at[d, i - 1, f], br.at[d, i - 1, f], at_z(-sgn[d] * i))

    def p_con(o, f):
        return rcopy(CP.at[o, :, cols(f)], CR.at[o, :, cols(f)], cs_.at[o, f], cr_.at[o, f], partner)

    def ring(d, j, f):
        return rcopy(C.at[idx(d, j), :, cols(f)], RZ.at[d, j - 1, :, cols(f)],
                     rs.at[d, j - 1, f], rr.at[d, j - 1, f], at_z(-sgn[d]))

    lane = lax.broadcasted_iota(jnp.int32, (1, 128), 1)

    def picks(o, n, first, scored):
        def both(r):
            return jnp.where(lane < rows, M[o, 0, r:r + 1, :], M[o, 1, r:r + 1, :])
        r = lax.broadcasted_iota(jnp.int32, (n * blk, 128), 0)
        ln = lax.broadcasted_iota(jnp.int32, (n * blk, 128), 1)
        ex = first(r // blk)
        ex = jnp.where(ex >= E, ex - E, ex)
        ex = jnp.where(ex < 0, ex + E, ex)
        slot = (cap * ex + lax.rem(r, cap)).astype(F32)
        mine = (lax.rem(r, blk) // cap) == (ln // rows)
        one = jnp.ones((n * blk, 128), F32)
        a, b = (both(2), both(3)) if scored else (one, one)
        val = jnp.where(both(0) == slot, a, 0.0) + jnp.where(both(1) == slot, b, 0.0)
        return jnp.where(mine, val, 0.0)[:, :2 * rows].astype(BF16)

    def own(o, scored):
        return picks(o, 1, lambda i: i + e, scored)

    def beyond(o, d, scored):
        return picks(o, HOP, lambda i: e + 2 * sgn[d] * (i + 1), scored)

    def select(lhs, o, f):
        return jnp.dot(lhs, T[o, :, :, cols(f)].reshape(2 * rows, fw), preferred_element_type=F32)

    kc = fw

    def ffn_in(b, f):
        n = NX * (b.stop - b.start) * blk
        lhs = G[:, b, :, cols(f)].reshape(n, fw)
        for m, W in ((0, WG), (1, WU)):
            got = jnp.dot(lhs, W[cols(f), :], preferred_element_type=F32)
            ACC[m, :, b] += got.reshape(NX, b.stop - b.start, blk, hid)

    def ffn_mid(b):
        gate = ACC[0, :, b]
        HID[:, b] = (gate / (1.0 + jnp.exp(-gate)) * ACC[1, :, b]).astype(BF16)

    def ffn_out(b, f):
        n = NX * (b.stop - b.start) * blk
        got = jnp.dot(HID[:, b].reshape(n, hid), WD[:, cols(f)], preferred_element_type=F32)
        PB[:, b, :, cols(f)] = got.astype(BF16).reshape(NX, b.stop - b.start, blk, fw)

    barrier = pltpu.get_barrier_semaphore()
    peers = [at_z(s * k) for k in range(1, HOP + 1) for s in sgn] + list(side_dev) + [partner]
    for dev in peers:
        pl.semaphore_signal(barrier, inc=1, device_id=dev, device_id_type=MESH)
    weights = [pltpu.make_async_copy(wg_in.at[0], WG, wsem.at[0]),
               pltpu.make_async_copy(wu_in.at[0], WU, wsem.at[1]),
               pltpu.make_async_copy(wd_in.at[0], WD, wsem.at[2])]
    for w in weights:
        w.start()

    row_t = lax.broadcasted_iota(jnp.int32, (rows, rows), 0)
    col_t = lax.broadcasted_iota(jnp.int32, (rows, rows), 1)
    named = [ids[k:k + 1, :].astype(F32) for k in (0, 1)]
    stood = [jnp.sum(jnp.where(row_t == col_t, r, 0.0), axis=1, keepdims=True) for r in named]
    M[0, 0] = jnp.zeros((8, 128), F32)
    for k in (0, 1):
        ahead = [jnp.where((q == named[k]) & (row_t < col_t), 1.0, 0.0) for q in stood]
        M[0, 0, k:k + 1, 0:rows] = named[k] * cap + jnp.sum(ahead[0] + ahead[1], axis=0, keepdims=True)
        M[0, 0, 2 + k:3 + k, 0:rows] = scores[k:k + 1, :]
    once = M[0, 0]
    M[0, 0] = jnp.where(lane < 2 * rows, once + pltpu.roll(once, rows, 1), -1.0)

    total = jnp.zeros((rows, 1), F32)
    for k in range(0, width, kc):
        t = tokens[:, k:k + kc].astype(F32)
        total = total + jnp.sum(t * t, axis=1, keepdims=True)
    scale = lax.rsqrt(total / width + 1e-05)
    for k in range(0, width, kc):
        T[0, 0, :, k:k + kc] = (tokens[:, k:k + kc].astype(F32) * scale * gain[:, k:k + kc]).astype(BF16)
    ACC[...] = jnp.zeros_like(ACC)
    FR[1 - c, HOP - 1] = jnp.zeros((blk, width), BF16)
    pl.semaphore_wait(barrier, len(peers))

    sent = []

    def go(make, *a):
        make(*a).start()
        sent.append((make, a))

    def weigh(lhs, rhs):
        return lax.dot_general(lhs, rhs, (((0,), (0,)), ((), ())), preferred_element_type=F32)

    seen = set()

    def new(*key):
        fresh = key not in seen
        seen.add(key)
        return fresh

    def launch(f):
        go(p_tok, 0, f)
        go(z_tok, 0, 0, f)
        go(z_tok, 1, 0, f)

    def hop(j, f):
        if new("hop", j):
            for d in (0, 1):
                z_meta(d, j - 1).wait_recv()
                if j < HOP:
                    go(z_meta, d, j)
                go(p_meta, idx(d, j))
        for d in (0, 1):
            z_tok(d, j - 1, f).wait_recv()
            if j < HOP:
                go(z_tok, d, j, f)
            go(p_tok, idx(d, j), f)

    def choose(j, f):
        for d in ((0, 1) if j > 0 else (0,)):
            o = idx(d, j)
            if new("choose", o):
                p_meta(o).wait_recv()
            lhs = own(o, False)
            if j == HOP:
                lhs = jnp.concatenate([lhs, beyond(o, d, False)], axis=0)
            p_tok(o, f).wait_recv()
            got = select(lhs, o, f).astype(BF16)
            G[0, o, :, cols(f)] = got[:blk]
            if j == HOP:
                FS[d, :, :, cols(f)] = got[blk:].reshape(HOP, blk, fw)
        if j == HOP:
            for i in range(1, HOP):
                for d in (0, 1):
                    go(far, d, i, f)
            go(far, 0, HOP, f)

    def spread(g, f):
        if g == FARG:
            for i in range(1, HOP):
                for d in (0, 1):
                    far(d, i, f).wait_recv()
            far(0, HOP, f).wait_recv()
        for side in (0, 1):
            go(xsend, g, f, side)

    def forward(g, f):
        for side in (0, 1):
            xsend(g, f, side).wait_recv()
            go(xfwd, g, f, side)

    def layer_in(q, f):
        if new("weights"):
            for w in weights:
                w.wait()
        for g in (range(FARG) if q == 0 else (FARG,)):
            for side in (0, 1):
                xfwd(g, f, side).wait_recv()
        ffn_in((nears, fars)[q], f)

    def layer_mid(q):
        ffn_mid((nears, fars)[q])

    def layer_out(q, f):
        ffn_out((nears, fars)[q], f)

    def begin(g, f):
        for side in (0, 1):
            go(opp, g, f, side)

    def middle(g, f):
        k = cols(f)
        for side in (0, 1):
            b = half(g, side)
            opp(g, f, side).wait_recv()
            PB[2 - side, b, :, k] = (PB[2 - side, b, :, k].astype(F32) + OPP[b, :, k].astype(F32)).astype(BF16)
            go(main, g, f, side)

    def finish(g, f):
        b, k = slice(*groups[g]), cols(f)
        for side in (0, 1):
            main(g, f, side).wait_recv()
        R[b, :, k] = (PB[0, b, :, k].astype(F32) + RX[0, b, :, k].astype(F32) + RX[1, b, :, k].astype(F32)).astype(BF16)
        if g == FARG:
            go(back, 0, HOP, f)
            for i in range(HOP - 1, 0, -1):
                for d in (0, 1):
                    go(back, d, i, f)

    def give(j, f):
        for d in ((0, 1) if j > 0 else (0,)):
            o = idx(d, j)
            u = weigh(own(o, True), R[o, :, cols(f)])
            if j == HOP:
                for i in range(1, HOP):
                    back(d, i, f).wait_recv()
                if d == 0:
                    back(0, HOP, f).wait_recv()
                u = u + weigh(beyond(o, d, True), FR[d, :, :, cols(f)].reshape(HOP * blk, fw))
            C[o, :, cols(f)] = u[:rows].astype(BF16)
            CP[o, :, cols(f)] = u[rows:].astype(BF16)
            go(p_con, o, f)

    def pass_on(j, f):
        for d in (0, 1):
            o = idx(d, j)
            p_con(o, f).wait_recv()
            v = C[o, :, cols(f)].astype(F32) + CR[o, :, cols(f)].astype(F32)
            if j < HOP:
                ring(d, j + 1, f).wait_recv()
                v = v + RZ[d, j, :, cols(f)].astype(F32)
            C[o, :, cols(f)] = v.astype(BF16)
            go(ring, d, j, f)

    def last(f):
        p_con(0, f).wait_recv()
        ring(0, 1, f).wait_recv()
        ring(1, 1, f).wait_recv()
        out[:, cols(f)] = (C[0, :, cols(f)].astype(F32) + CR[0, :, cols(f)].astype(F32)
                           + RZ[0, 0, :, cols(f)].astype(F32) + RZ[1, 0, :, cols(f)].astype(F32)).astype(BF16)

    for d in (0, 1):
        go(z_meta, d, 0)
    go(p_meta, 0)
    run = {"L": launch, "H": hop, "S": choose, "X": spread, "XF": forward, "FI": layer_in, "FM": layer_mid,
           "FO": layer_out, "O": begin, "M": middle, "N": finish, "G": give, "P": pass_on, "E": last}
    for task in ORDER:
        with jax.named_scope("_".join(map(str, task))):
            run[task[0]](*task[1:])
    for make, a in sent:
        make(*a).wait_send()


def on_device(tokens, expert_ids, gate_scores, norm_gain, w_gate, w_up, w_down):
    rows, width = tokens.shape
    E, NX = lax.axis_size("expert"), lax.axis_size("tensor")
    cap = 4 * rows // E
    Z, HOP, blk, hid = E // 2, E // 8, 2 * cap, w_gate.shape[2]
    NG, NO = 4 * PARTS, 2 * HOP + 1
    v = lambda *s: pltpu.VMEM(s, BF16)
    return pl.pallas_call(
        functools.partial(kernel, E, NX, rows, width),
        out_shape=jax.ShapeDtypeStruct((rows, width), BF16),
        in_specs=[pl.BlockSpec(memory_space=pltpu.VMEM)] * 4 + [pl.BlockSpec(memory_space=pl.ANY)] * 3,
        out_specs=pl.BlockSpec(memory_space=pltpu.VMEM),
        scratch_shapes=[
            v(NO, 2, rows, width),
            pltpu.VMEM((NO, 2, 8, 128), F32),
            v(2, HOP, blk, width),
            v(NX, Z, blk, width),
            v(width, hid), v(width, hid), v(hid, width),
            pltpu.VMEM((2, NX, Z, blk, hid), F32),
            v(NX, Z, blk, hid),
            v(NX, Z, blk, width),
            v(Z, blk, width),
            v(2, Z, blk, width),
            v(Z, blk, width),
            v(2, HOP, blk, width),
            v(NO, rows, width), v(NO, rows, width), v(NO, rows, width),
            v(2, HOP, rows, width),
            DMA((3,)),
            DMA((2, HOP, PARTS)), DMA((2, HOP, PARTS)), DMA((NO, PARTS)), DMA((NO, PARTS)),
            DMA((2, HOP)), DMA((2, HOP)), DMA((NO,)), DMA((NO,)),
            DMA((2, HOP, PARTS)), DMA((2, HOP, PARTS)),
            DMA((NG, 2)), DMA((NG, 2)), DMA((NG, 2)), DMA((NG, 2)),
            DMA((NG, 2)), DMA((NG, 2)), DMA((NG, 2)), DMA((NG, 2)),
            DMA((2, HOP, PARTS)), DMA((2, HOP, PARTS)),
            DMA((NO, PARTS)), DMA((NO, PARTS)),
            DMA((2, HOP, PARTS)), DMA((2, HOP, PARTS)),
        ],
        compiler_params=pltpu.CompilerParams(collective_id=0, has_side_effects=True, vmem_limit_bytes=63 * 1024 * 1024),
    )(tokens, expert_ids.T, gate_scores.T, norm_gain.reshape(1, width), w_gate, w_up, w_down)


def solution(mesh):
    return jax.shard_map(
        on_device,
        mesh=mesh,
        in_specs=(
            P(("groups", "expert", "tensor"), None),
            P(("groups", "expert", "tensor"), None),
            P(("groups", "expert", "tensor"), None),
            P(),
            P("expert", None, "tensor"),
            P("expert", None, "tensor"),
            P("expert", "tensor", None),
        ),
        out_specs=P(("groups", "expert", "tensor"), None),
        check_vma=False,
    )
```

time: 382 us -> 176 us (0.46)
  blocking collectives: 195 us -> 0 us
  Pallas kernels: 0 us -> 173 us
  waiting for transfers between devices: 135 us -> 0 us
  matrix products: 17.2 us -> 0 us
  local copies, waits for them, and re-layouts: 16.7 us -> 1.77 us
  between operations: 13.5 us -> 0.01 us
    all_to_all x2 -> x0, blocking collectives: 195 us -> none  [the longest x1 104 us: on_device(): lax.all_to_all(outgoing, 'expert', split_axis=0, concat_axis=0, tiled=True)]
    pallas_call x0 -> x1, Pallas kernels: none -> 173 us  [on_device(): pl.pallas_call(functools.partial(kernel, E, NX, rows, width), out_shape=j...]
    reduce_scatter x1 -> x0, waiting for transfers between devices: 71 us -> none  [on_device(): lax.psum_scatter(parts.astype(jnp.bfloat16), 'tensor', scatter_dimension=...]
    all_gather x1 -> x0, waiting for transfers between devices: 63.8 us -> none  [on_device(): piece = lax.all_gather(arrived, 'tensor', axis=0, tiled=True)]
    dot_general x5 -> x0, matrix products: 17.2 us -> none  [the longest x1 5.64 us: on_device(): gate = jnp.dot(piece, w_gate[0], preferred_element_type=jnp.float32)]
    reshape x4 -> x0, local copies, waits for them, and re-layouts: 14.9 us -> none  [the longest x1 3.81 us: on_device(): summed = summed.reshape(experts, capacity, width)]
  transfers between devices with their start and end apart: 2 -> 0, of which waited for: 2 -> 0; matrix products, arithmetic and copies ran while one was open for 0% -> 0% of each run, Pallas kernels for 0% -> 0%
where the time goes in v4:
time: 176 us; the launch traced here: 175 us
  Pallas kernels  173 us (98%)
  local copies, waits for them, and re-layouts  1.77 us (1%)
    pallas_call x1, Pallas kernels, on_device(): pl.pallas_call(functools.partial(kernel, E, NX, rows, width), out_shape=j...  173 us

profile of v4, /device:TPU:33, one launch (start us, length us, event | category | flops | bytes accessed | tf_op | source)
XLA Modules:
  0.0 175.2 jit_solution(1963845479956284827)
XLA Ops:
  0.0 173.5 %shard_map.73 = bf16[32,6144]{1,0:T(8,128)(2,1)} custom-call(bf16[32,6144]{1,0:T(8,128)(2,1)} %tokens.1, s32[2,32]{1,0:T(2,128)} %bitcast.4, f32[2,32]{1,0:T(2,128)} %bitcast.5, f32[1,6144]{1,0:T(1,128)} %bitcast.3, bf16[1,6144,256]{2,1,0:T(8,128)(2,1)} %wg_in.1, bf16[1,6144,256]{2,1,0:T(8,128)(2,1)} %wu_in.1, bf16[1,256,6144]{2,1,0:T(8,128)(2,1)} %wd_in.1), custom_call_target="tpu_custom_call" | custom-call | tf_op jit(solution)/shard_map/pallas_call | solution.py:365
  173.5 1.8 %copy.9 = bf16[32,6144]{1,0:T(8,128)(2,1)} copy(bf16[32,6144]{1,0:T(8,128)(2,1)} %shard_map.73) | data formatting | bytes 786432

commit v5 on v4

--- a/solution.py
+++ b/solution.py
@@ -9,31 +9,48 @@
 
 MESH = pl.DeviceIdType.MESH
 F32, BF16 = jnp.float32, jnp.bfloat16
-PARTS = 4
+SHARES = (10, 10, 10, 8, 6, 4)
+PARTS = len(SHARES)
+GROUPS = ((0, 3), (3, 7), (7, 9), (9, 13), (13, 16))
 DMA = pltpu.SemaphoreType.DMA
 ORDER = [
-    ("L", 0), ("L", 1), ("S", 0, 0), ("L", 2), ("S", 0, 1), ("S", 0, 2), ("L", 3), ("H", 1, 0), ("S", 0, 3),
-    ("S", 1, 0), ("X", 0, 0), ("H", 1, 1), ("S", 1, 1), ("X", 0, 1), ("H", 1, 2), ("XF", 0, 0), ("S", 1, 2),
-    ("X", 0, 2), ("H", 1, 3), ("XF", 0, 1), ("S", 1, 3), ("X", 0, 3), ("H", 2, 0), ("S", 2, 0), ("XF", 0, 2),
-    ("H", 2, 1), ("S", 2, 1), ("XF", 0, 3), ("H", 2, 2), ("S", 2, 2), ("H", 2, 3), ("S", 2, 3), ("H", 3, 0),
-    ("S", 3, 0), ("X", 1, 0), ("H", 3, 1), ("S", 3, 1), ("X", 1, 1), ("H", 3, 2), ("S", 3, 2), ("X", 1, 2),
-    ("XF", 1, 0), ("H", 3, 3), ("S", 3, 3), ("X", 1, 3), ("XF", 1, 1), ("H", 4, 0), ("S", 4, 0), ("X", 2, 0),
-    ("XF", 1, 2), ("H", 4, 1), ("S", 4, 1), ("X", 2, 1), ("H", 4, 2), ("XF", 1, 3), ("S", 4, 2), ("X", 2, 2),
-    ("H", 4, 3), ("XF", 2, 0), ("S", 4, 3), ("X", 2, 3), ("XF", 2, 1), ("XF", 2, 2), ("FI", 0, 0), ("X", 3, 0),
-    ("XF", 2, 3), ("FI", 0, 1), ("FI", 0, 2), ("X", 3, 1), ("XF", 3, 0), ("FI", 0, 3), ("FM", 0), ("FO", 0, 0),
-    ("FO", 0, 1), ("X", 3, 2), ("FO", 0, 2), ("FO", 0, 3), ("XF", 3, 1), ("FI", 1, 0), ("X", 3, 3), ("XF", 3, 2),
-    ("FI", 1, 1), ("O", 2, 0), ("O", 1, 0), ("XF", 3, 3), ("FI", 1, 2), ("O", 0, 0), ("M", 2, 0), ("M", 1, 0),
-    ("FI", 1, 3), ("FM", 1), ("M", 0, 0), ("FO", 1, 0), ("FO", 1, 1), ("N", 2, 0), ("FO", 1, 2), ("FO", 1, 3),
-    ("O", 3, 0), ("N", 1, 0), ("G", 3, 0), ("G", 2, 0), ("O", 3, 1), ("N", 0, 0), ("G", 1, 0), ("G", 0, 0),
-    ("O", 3, 2), ("M", 3, 0), ("M", 3, 1), ("M", 3, 2), ("N", 3, 0), ("N", 3, 1), ("O", 2, 1), ("O", 1, 1),
-    ("O", 0, 1), ("O", 3, 3), ("G", 4, 0), ("N", 3, 2), ("M", 2, 1), ("P", 4, 0), ("M", 1, 1), ("M", 0, 1),
-    ("M", 3, 3), ("N", 2, 1), ("G", 4, 1), ("P", 4, 1), ("N", 1, 1), ("G", 3, 1), ("G", 2, 1), ("N", 0, 1),
-    ("G", 1, 1), ("G", 0, 1), ("O", 2, 2), ("P", 3, 0), ("O", 1, 2), ("O", 0, 2), ("O", 2, 3), ("P", 3, 1),
-    ("O", 1, 3), ("N", 3, 3), ("M", 2, 2), ("M", 1, 2), ("P", 2, 0), ("M", 0, 2), ("M", 2, 3), ("P", 2, 1),
-    ("M", 1, 3), ("N", 2, 2), ("G", 4, 2), ("P", 4, 2), ("N", 1, 2), ("G", 3, 2), ("G", 2, 2), ("O", 0, 3),
-    ("N", 0, 2), ("G", 1, 2), ("G", 0, 2), ("N", 2, 3), ("G", 4, 3), ("P", 1, 0), ("P", 4, 3), ("N", 1, 3),
-    ("G", 3, 3), ("P", 1, 1), ("G", 2, 3), ("M", 0, 3), ("P", 3, 2), ("E", 0), ("N", 0, 3), ("G", 1, 3), ("G", 0, 3),
-    ("P", 3, 3), ("E", 1), ("P", 2, 2), ("P", 2, 3), ("P", 1, 2), ("P", 1, 3), ("E", 2), ("E", 3),
+    ("L", 1), ("L", 3), ("S", 0, 1), ("S", 0, 3), ("L", 0), ("S", 0, 0), ("H", 1, 1), ("S", 1, 1), ("H", 1, 3),
+    ("X", 0, 1), ("S", 1, 3), ("X", 0, 3), ("H", 1, 0), ("S", 1, 0), ("X", 0, 0), ("H", 2, 1), ("XF", 0, 1),
+    ("S", 2, 1), ("H", 2, 3), ("XF", 0, 3), ("S", 2, 3), ("H", 2, 0), ("XF", 0, 0), ("S", 2, 0), ("H", 3, 1),
+    ("S", 3, 1), ("H", 3, 3), ("X", 1, 1), ("S", 3, 3), ("X", 1, 3), ("H", 3, 0), ("S", 3, 0), ("X", 1, 0),
+    ("H", 4, 1), ("L", 4), ("XF", 1, 1), ("L", 2), ("S", 4, 1), ("H", 4, 3), ("S", 0, 4), ("X", 2, 1), ("XF", 1, 3),
+    ("S", 0, 2), ("S", 4, 3), ("H", 4, 0), ("X", 2, 3), ("XF", 1, 0), ("H", 1, 4), ("S", 4, 0), ("X", 2, 0),
+    ("S", 1, 4), ("X", 0, 4), ("XF", 2, 1), ("H", 1, 2), ("XF", 2, 3), ("S", 1, 2), ("X", 0, 2), ("X", 3, 1),
+    ("XF", 2, 0), ("XF", 0, 4), ("FI", 0, 1), ("FI", 0, 3), ("X", 3, 3), ("X", 4, 1), ("XF", 0, 2), ("H", 2, 4),
+    ("XF", 3, 1), ("FI", 0, 0), ("X", 4, 3), ("S", 2, 4), ("X", 3, 0), ("XF", 3, 3), ("L", 5), ("XF", 4, 1),
+    ("S", 0, 5), ("H", 2, 2), ("X", 4, 0), ("H", 3, 4), ("XF", 4, 3), ("S", 2, 2), ("H", 1, 5), ("S", 3, 4),
+    ("X", 1, 4), ("XF", 3, 0), ("S", 1, 5), ("X", 0, 5), ("H", 3, 2), ("FI", 1, 1), ("H", 4, 4), ("S", 3, 2),
+    ("XF", 4, 0), ("X", 1, 2), ("H", 2, 5), ("FI", 1, 3), ("S", 4, 4), ("X", 2, 4), ("S", 2, 5), ("XF", 1, 4),
+    ("H", 4, 2), ("XF", 0, 5), ("H", 3, 5), ("FI", 1, 0), ("S", 4, 2), ("X", 2, 2), ("S", 3, 5), ("X", 1, 5),
+    ("X", 3, 4), ("XF", 1, 2), ("XF", 2, 4), ("H", 4, 5), ("X", 4, 4), ("XF", 2, 2), ("S", 4, 5), ("X", 2, 5),
+    ("XF", 1, 5), ("X", 3, 2), ("XF", 3, 4), ("FI", 0, 4), ("XF", 4, 4), ("X", 3, 5), ("FI", 0, 2), ("XF", 2, 5),
+    ("X", 4, 2), ("X", 4, 5), ("XF", 3, 2), ("FI", 1, 4), ("XF", 3, 5), ("FI", 0, 5), ("FM", 0), ("FO", 0, 0),
+    ("O", 2, 0), ("FO", 0, 1), ("O", 2, 1), ("FO", 0, 2), ("XF", 4, 2), ("FO", 0, 3), ("FO", 0, 4), ("XF", 4, 5),
+    ("FO", 0, 5), ("O", 2, 4), ("O", 1, 0), ("M", 2, 0), ("M", 2, 1), ("FI", 1, 2), ("FI", 1, 5), ("FM", 1),
+    ("M", 2, 4), ("FO", 1, 0), ("FO", 1, 1), ("O", 4, 0), ("FO", 1, 2), ("M", 1, 0), ("FO", 1, 3), ("FO", 1, 4),
+    ("FO", 1, 5), ("N", 2, 0), ("N", 2, 1), ("O", 3, 0), ("N", 2, 4), ("M", 4, 0), ("O", 4, 3), ("N", 1, 0),
+    ("G", 3, 0), ("O", 4, 1), ("G", 2, 0), ("M", 3, 0), ("N", 4, 0), ("O", 3, 1), ("M", 4, 3), ("M", 4, 1),
+    ("N", 3, 0), ("O", 3, 2), ("M", 3, 1), ("N", 4, 3), ("N", 4, 1), ("O", 3, 4), ("O", 3, 3), ("G", 4, 0),
+    ("M", 3, 2), ("P", 4, 0), ("N", 3, 1), ("O", 4, 2), ("M", 3, 4), ("M", 3, 3), ("N", 3, 2), ("O", 4, 5),
+    ("M", 4, 2), ("P", 3, 0), ("N", 3, 4), ("O", 4, 4), ("O", 3, 5), ("G", 4, 1), ("N", 3, 3), ("O", 2, 3),
+    ("M", 4, 5), ("O", 1, 1), ("P", 4, 1), ("N", 4, 2), ("O", 2, 2), ("M", 4, 4), ("M", 3, 5), ("P", 2, 0),
+    ("M", 2, 3), ("N", 4, 5), ("M", 1, 1), ("M", 2, 2), ("N", 4, 4), ("N", 3, 5), ("N", 2, 3), ("G", 4, 3),
+    ("O", 2, 5), ("O", 1, 4), ("O", 0, 0), ("O", 1, 5), ("P", 4, 3), ("N", 1, 1), ("G", 2, 1), ("G", 3, 1),
+    ("O", 1, 2), ("N", 2, 2), ("G", 4, 2), ("M", 2, 5), ("O", 1, 3), ("M", 1, 4), ("P", 3, 1), ("M", 0, 0),
+    ("M", 1, 5), ("P", 4, 2), ("M", 1, 2), ("N", 2, 5), ("G", 4, 5), ("M", 1, 3), ("G", 4, 4), ("P", 4, 5),
+    ("N", 1, 4), ("G", 3, 4), ("G", 2, 4), ("P", 4, 4), ("N", 0, 0), ("G", 1, 0), ("P", 2, 1), ("G", 0, 0),
+    ("N", 1, 5), ("G", 3, 5), ("G", 2, 5), ("O", 0, 4), ("P", 1, 0), ("O", 0, 5), ("O", 0, 2), ("N", 1, 2),
+    ("P", 3, 5), ("G", 3, 2), ("G", 2, 2), ("O", 0, 1), ("P", 3, 4), ("O", 0, 3), ("N", 1, 3), ("G", 2, 3),
+    ("P", 3, 2), ("G", 3, 3), ("M", 0, 4), ("M", 0, 5), ("M", 0, 2), ("P", 3, 3), ("M", 0, 1), ("M", 0, 3), ("E", 0),
+    ("N", 0, 4), ("G", 1, 4), ("G", 0, 4), ("P", 2, 5), ("N", 0, 5), ("G", 0, 5), ("G", 1, 5), ("P", 2, 4),
+    ("N", 0, 2), ("G", 0, 2), ("G", 1, 2), ("P", 2, 2), ("N", 0, 1), ("G", 1, 1), ("G", 0, 1), ("N", 0, 3),
+    ("G", 0, 3), ("G", 1, 3), ("P", 2, 3), ("P", 1, 1), ("P", 1, 5), ("P", 1, 4), ("P", 1, 2), ("P", 1, 3), ("E", 1),
+    ("E", 5), ("E", 4), ("E", 2), ("E", 3),
 ]
 
 
@@ -45,7 +62,7 @@
     HOP = Z // 4
     cap = 4 * rows // E
     blk = 2 * cap
-    fw = width // PARTS
+    unit = width // sum(SHARES)
     hid = WG.shape[1]
     e = lax.axis_index("expert")
     x = lax.axis_index("tensor")
@@ -59,7 +76,7 @@
     side_dev = ({"tensor": lax.rem(x + 1, NX)}, {"tensor": lax.rem(x + NX - 1, NX)})
 
     def cols(f):
-        return slice(f * fw, (f + 1) * fw)
+        return slice(unit * sum(SHARES[:f]), unit * sum(SHARES[:f + 1]))
 
     def rcopy(src, dst, s, r, dev):
         return pltpu.make_async_remote_copy(src_ref=src, dst_ref=dst, send_sem=s, recv_sem=r,
@@ -90,13 +107,17 @@
                      fs.at[d, i - 1, f], fr.at[d, i - 1, f], at_z(sgn[d] * i))
 
     mid, NB = 2 * HOP + 1, Z
-    groups = [(0, 3), (3, 2 * HOP - 1), (2 * HOP - 1, mid), (mid, NB)]
-    FARG = len(groups) - 1
+    groups = GROUPS
+    near_g = [g for g in range(len(groups)) if groups[g][0] < mid]
+    far_g = [g for g in range(len(groups)) if groups[g][0] >= mid]
     nears, fars = slice(0, mid), slice(mid, NB)
+
+    def relayed(g):
+        return [i for i in range(1, HOP + 1) if groups[g][0] <= 2 * (HOP + i) - 1 < groups[g][1]]
 
     def half(g, side):
         b0, b1 = groups[g]
-        cut = (b0 + b1 + (g == FARG)) // 2
+        cut = (b0 + b1 + (b0 >= mid)) // 2
         return slice(b0, cut) if side == 0 else slice(cut, b1)
 
     def xsend(g, f, side):
@@ -153,13 +174,13 @@
         return picks(o, HOP, lambda i: e + 2 * sgn[d] * (i + 1), scored)
 
     def select(lhs, o, f):
-        return jnp.dot(lhs, T[o, :, :, cols(f)].reshape(2 * rows, fw), preferred_element_type=F32)
-
-    kc = fw
+        return jnp.dot(lhs, T[o, :, :, cols(f)].reshape(2 * rows, -1), preferred_element_type=F32)
+
+    kc = width // 6
 
     def ffn_in(b, f):
         n = NX * (b.stop - b.start) * blk
-        lhs = G[:, b, :, cols(f)].reshape(n, fw)
+        lhs = G[:, b, :, cols(f)].reshape(n, -1)
         for m, W in ((0, WG), (1, WU)):
             got = jnp.dot(lhs, W[cols(f), :], preferred_element_type=F32)
             ACC[m, :, b] += got.reshape(NX, b.stop - b.start, blk, hid)
@@ -171,7 +192,7 @@
     def ffn_out(b, f):
         n = NX * (b.stop - b.start) * blk
         got = jnp.dot(HID[:, b].reshape(n, hid), WD[:, cols(f)], preferred_element_type=F32)
-        PB[:, b, :, cols(f)] = got.astype(BF16).reshape(NX, b.stop - b.start, blk, fw)
+        PB[:, b, :, cols(f)] = got.astype(BF16).reshape(NX, b.stop - b.start, blk, -1)
 
     barrier = pltpu.get_barrier_semaphore()
     peers = [at_z(s * k) for k in range(1, HOP + 1) for s in sgn] + list(side_dev) + [partner]
@@ -252,7 +273,7 @@
             got = select(lhs, o, f).astype(BF16)
             G[0, o, :, cols(f)] = got[:blk]
             if j == HOP:
-                FS[d, :, :, cols(f)] = got[blk:].reshape(HOP, blk, fw)
+                FS[d, :, :, cols(f)] = got[blk:].reshape(HOP, blk, -1)
         if j == HOP:
             for i in range(1, HOP):
                 for d in (0, 1):
@@ -260,11 +281,10 @@
             go(far, 0, HOP, f)
 
     def spread(g, f):
-        if g == FARG:
-            for i in range(1, HOP):
-                for d in (0, 1):
+        if g in far_g:
+            for i in relayed(g):
+                for d in ((0, 1) if i < HOP else (0,)):
                     far(d, i, f).wait_recv()
-            far(0, HOP, f).wait_recv()
         for side in (0, 1):
             go(xsend, g, f, side)
 
@@ -277,7 +297,7 @@
         if new("weights"):
             for w in weights:
                 w.wait()
-        for g in (range(FARG) if q == 0 else (FARG,)):
+        for g in (near_g, far_g)[q]:
             for side in (0, 1):
                 xfwd(g, f, side).wait_recv()
         ffn_in((nears, fars)[q], f)
@@ -305,10 +325,9 @@
         for side in (0, 1):
             main(g, f, side).wait_recv()
         R[b, :, k] = (PB[0, b, :, k].astype(F32) + RX[0, b, :, k].astype(F32) + RX[1, b, :, k].astype(F32)).astype(BF16)
-        if g == FARG:
-            go(back, 0, HOP, f)
-            for i in range(HOP - 1, 0, -1):
-                for d in (0, 1):
+        if g in far_g:
+            for i in relayed(g)[::-1]:
+                for d in ((0, 1) if i < HOP else (0,)):
                     go(back, d, i, f)
 
     def give(j, f):
@@ -320,7 +339,7 @@
                     back(d, i, f).wait_recv()
                 if d == 0:
                     back(0, HOP, f).wait_recv()
-                u = u + weigh(beyond(o, d, True), FR[d, :, :, cols(f)].reshape(HOP * blk, fw))
+                u = u + weigh(beyond(o, d, True), FR[d, :, :, cols(f)].reshape(HOP * blk, -1))
             C[o, :, cols(f)] = u[:rows].astype(BF16)
             CP[o, :, cols(f)] = u[rows:].astype(BF16)
             go(p_con, o, f)
@@ -360,7 +379,7 @@
     E, NX = lax.axis_size("expert"), lax.axis_size("tensor")
     cap = 4 * rows // E
     Z, HOP, blk, hid = E // 2, E // 8, 2 * cap, w_gate.shape[2]
-    NG, NO = 4 * PARTS, 2 * HOP + 1
+    NG, NO = len(GROUPS) * PARTS, 2 * HOP + 1
     v = lambda *s: pltpu.VMEM(s, BF16)
     return pl.pallas_call(
         functools.partial(kernel, E, NX, rows, width),

time: 176 us -> 173 us (0.983)
  Pallas kernels: 173 us -> 171 us
    pallas_call x1, Pallas kernels: 173 us -> 171 us  [on_device(): pl.pallas_call(functools.partial(kernel, E, NX, rows, width), out_shape=j...]
where the time goes in v5:
time: 173 us
  Pallas kernels  171 us (99%)
  local copies, waits for them, and re-layouts  1.77 us (1%)
    pallas_call x1, Pallas kernels, on_device(): pl.pallas_call(functools.partial(kernel, E, NX, rows, width), out_shape=j...  171 us

profile of v5, /device:TPU:33, one launch (start us, length us, event | category | flops | bytes accessed | tf_op | source)
XLA Modules:
  0.0 173.2 jit_solution(15071198961867689565)
XLA Ops:
  0.0 171.4 %shard_map.73 = bf16[32,6144]{1,0:T(8,128)(2,1)} custom-call(bf16[32,6144]{1,0:T(8,128)(2,1)} %tokens.1, s32[2,32]{1,0:T(2,128)} %bitcast.4, f32[2,32]{1,0:T(2,128)} %bitcast.5, f32[1,6144]{1,0:T(1,128)} %bitcast.3, bf16[1,6144,256]{2,1,0:T(8,128)(2,1)} %wg_in.1, bf16[1,6144,256]{2,1,0:T(8,128)(2,1)} %wu_in.1, bf16[1,256,6144]{2,1,0:T(8,128)(2,1)} %wd_in.1), custom_call_target="tpu_custom_call" | custom-call | tf_op jit(solution)/shard_map/pallas_call | solution.py:384
  171.4 1.8 %copy.9 = bf16[32,6144]{1,0:T(8,128)(2,1)} copy(bf16[32,6144]{1,0:T(8,128)(2,1)} %shard_map.73) | data formatting | bytes 786432

commit v6 on v5

--- a/solution.py
+++ b/solution.py
@@ -9,48 +9,48 @@
 
 MESH = pl.DeviceIdType.MESH
 F32, BF16 = jnp.float32, jnp.bfloat16
-SHARES = (10, 10, 10, 8, 6, 4)
+SHARES = (9, 9, 9, 9, 7, 5)
 PARTS = len(SHARES)
 GROUPS = ((0, 3), (3, 7), (7, 9), (9, 13), (13, 16))
 DMA = pltpu.SemaphoreType.DMA
 ORDER = [
-    ("L", 1), ("L", 3), ("S", 0, 1), ("S", 0, 3), ("L", 0), ("S", 0, 0), ("H", 1, 1), ("S", 1, 1), ("H", 1, 3),
-    ("X", 0, 1), ("S", 1, 3), ("X", 0, 3), ("H", 1, 0), ("S", 1, 0), ("X", 0, 0), ("H", 2, 1), ("XF", 0, 1),
-    ("S", 2, 1), ("H", 2, 3), ("XF", 0, 3), ("S", 2, 3), ("H", 2, 0), ("XF", 0, 0), ("S", 2, 0), ("H", 3, 1),
-    ("S", 3, 1), ("H", 3, 3), ("X", 1, 1), ("S", 3, 3), ("X", 1, 3), ("H", 3, 0), ("S", 3, 0), ("X", 1, 0),
-    ("H", 4, 1), ("L", 4), ("XF", 1, 1), ("L", 2), ("S", 4, 1), ("H", 4, 3), ("S", 0, 4), ("X", 2, 1), ("XF", 1, 3),
-    ("S", 0, 2), ("S", 4, 3), ("H", 4, 0), ("X", 2, 3), ("XF", 1, 0), ("H", 1, 4), ("S", 4, 0), ("X", 2, 0),
-    ("S", 1, 4), ("X", 0, 4), ("XF", 2, 1), ("H", 1, 2), ("XF", 2, 3), ("S", 1, 2), ("X", 0, 2), ("X", 3, 1),
-    ("XF", 2, 0), ("XF", 0, 4), ("FI", 0, 1), ("FI", 0, 3), ("X", 3, 3), ("X", 4, 1), ("XF", 0, 2), ("H", 2, 4),
-    ("XF", 3, 1), ("FI", 0, 0), ("X", 4, 3), ("S", 2, 4), ("X", 3, 0), ("XF", 3, 3), ("L", 5), ("XF", 4, 1),
-    ("S", 0, 5), ("H", 2, 2), ("X", 4, 0), ("H", 3, 4), ("XF", 4, 3), ("S", 2, 2), ("H", 1, 5), ("S", 3, 4),
-    ("X", 1, 4), ("XF", 3, 0), ("S", 1, 5), ("X", 0, 5), ("H", 3, 2), ("FI", 1, 1), ("H", 4, 4), ("S", 3, 2),
-    ("XF", 4, 0), ("X", 1, 2), ("H", 2, 5), ("FI", 1, 3), ("S", 4, 4), ("X", 2, 4), ("S", 2, 5), ("XF", 1, 4),
-    ("H", 4, 2), ("XF", 0, 5), ("H", 3, 5), ("FI", 1, 0), ("S", 4, 2), ("X", 2, 2), ("S", 3, 5), ("X", 1, 5),
-    ("X", 3, 4), ("XF", 1, 2), ("XF", 2, 4), ("H", 4, 5), ("X", 4, 4), ("XF", 2, 2), ("S", 4, 5), ("X", 2, 5),
-    ("XF", 1, 5), ("X", 3, 2), ("XF", 3, 4), ("FI", 0, 4), ("XF", 4, 4), ("X", 3, 5), ("FI", 0, 2), ("XF", 2, 5),
-    ("X", 4, 2), ("X", 4, 5), ("XF", 3, 2), ("FI", 1, 4), ("XF", 3, 5), ("FI", 0, 5), ("FM", 0), ("FO", 0, 0),
-    ("O", 2, 0), ("FO", 0, 1), ("O", 2, 1), ("FO", 0, 2), ("XF", 4, 2), ("FO", 0, 3), ("FO", 0, 4), ("XF", 4, 5),
-    ("FO", 0, 5), ("O", 2, 4), ("O", 1, 0), ("M", 2, 0), ("M", 2, 1), ("FI", 1, 2), ("FI", 1, 5), ("FM", 1),
-    ("M", 2, 4), ("FO", 1, 0), ("FO", 1, 1), ("O", 4, 0), ("FO", 1, 2), ("M", 1, 0), ("FO", 1, 3), ("FO", 1, 4),
-    ("FO", 1, 5), ("N", 2, 0), ("N", 2, 1), ("O", 3, 0), ("N", 2, 4), ("M", 4, 0), ("O", 4, 3), ("N", 1, 0),
-    ("G", 3, 0), ("O", 4, 1), ("G", 2, 0), ("M", 3, 0), ("N", 4, 0), ("O", 3, 1), ("M", 4, 3), ("M", 4, 1),
-    ("N", 3, 0), ("O", 3, 2), ("M", 3, 1), ("N", 4, 3), ("N", 4, 1), ("O", 3, 4), ("O", 3, 3), ("G", 4, 0),
-    ("M", 3, 2), ("P", 4, 0), ("N", 3, 1), ("O", 4, 2), ("M", 3, 4), ("M", 3, 3), ("N", 3, 2), ("O", 4, 5),
-    ("M", 4, 2), ("P", 3, 0), ("N", 3, 4), ("O", 4, 4), ("O", 3, 5), ("G", 4, 1), ("N", 3, 3), ("O", 2, 3),
-    ("M", 4, 5), ("O", 1, 1), ("P", 4, 1), ("N", 4, 2), ("O", 2, 2), ("M", 4, 4), ("M", 3, 5), ("P", 2, 0),
-    ("M", 2, 3), ("N", 4, 5), ("M", 1, 1), ("M", 2, 2), ("N", 4, 4), ("N", 3, 5), ("N", 2, 3), ("G", 4, 3),
-    ("O", 2, 5), ("O", 1, 4), ("O", 0, 0), ("O", 1, 5), ("P", 4, 3), ("N", 1, 1), ("G", 2, 1), ("G", 3, 1),
-    ("O", 1, 2), ("N", 2, 2), ("G", 4, 2), ("M", 2, 5), ("O", 1, 3), ("M", 1, 4), ("P", 3, 1), ("M", 0, 0),
-    ("M", 1, 5), ("P", 4, 2), ("M", 1, 2), ("N", 2, 5), ("G", 4, 5), ("M", 1, 3), ("G", 4, 4), ("P", 4, 5),
-    ("N", 1, 4), ("G", 3, 4), ("G", 2, 4), ("P", 4, 4), ("N", 0, 0), ("G", 1, 0), ("P", 2, 1), ("G", 0, 0),
-    ("N", 1, 5), ("G", 3, 5), ("G", 2, 5), ("O", 0, 4), ("P", 1, 0), ("O", 0, 5), ("O", 0, 2), ("N", 1, 2),
-    ("P", 3, 5), ("G", 3, 2), ("G", 2, 2), ("O", 0, 1), ("P", 3, 4), ("O", 0, 3), ("N", 1, 3), ("G", 2, 3),
-    ("P", 3, 2), ("G", 3, 3), ("M", 0, 4), ("M", 0, 5), ("M", 0, 2), ("P", 3, 3), ("M", 0, 1), ("M", 0, 3), ("E", 0),
-    ("N", 0, 4), ("G", 1, 4), ("G", 0, 4), ("P", 2, 5), ("N", 0, 5), ("G", 0, 5), ("G", 1, 5), ("P", 2, 4),
-    ("N", 0, 2), ("G", 0, 2), ("G", 1, 2), ("P", 2, 2), ("N", 0, 1), ("G", 1, 1), ("G", 0, 1), ("N", 0, 3),
-    ("G", 0, 3), ("G", 1, 3), ("P", 2, 3), ("P", 1, 1), ("P", 1, 5), ("P", 1, 4), ("P", 1, 2), ("P", 1, 3), ("E", 1),
-    ("E", 5), ("E", 4), ("E", 2), ("E", 3),
+    ("L", 0), ("L", 2), ("S", 0, 0), ("S", 0, 2), ("L", 1), ("S", 0, 1), ("H", 1, 0), ("S", 1, 0), ("X", 0, 0),
+    ("H", 1, 2), ("S", 1, 2), ("X", 0, 2), ("H", 1, 1), ("S", 1, 1), ("X", 0, 1), ("H", 2, 0), ("XF", 0, 0),
+    ("S", 2, 0), ("H", 2, 2), ("XF", 0, 2), ("S", 2, 2), ("H", 2, 1), ("XF", 0, 1), ("S", 2, 1), ("H", 3, 0),
+    ("S", 3, 0), ("X", 1, 0), ("H", 3, 2), ("S", 3, 2), ("X", 1, 2), ("H", 3, 1), ("S", 3, 1), ("X", 1, 1),
+    ("H", 4, 0), ("L", 3), ("XF", 1, 0), ("S", 4, 0), ("H", 4, 2), ("S", 0, 3), ("X", 2, 0), ("XF", 1, 2),
+    ("S", 4, 2), ("H", 4, 1), ("X", 2, 2), ("XF", 1, 1), ("H", 1, 3), ("S", 4, 1), ("X", 2, 1), ("XF", 2, 0),
+    ("S", 1, 3), ("X", 0, 3), ("X", 3, 0), ("XF", 2, 2), ("XF", 2, 1), ("FI", 0, 0), ("X", 3, 2), ("X", 4, 0),
+    ("XF", 0, 3), ("XF", 3, 0), ("FI", 0, 2), ("H", 2, 3), ("FI", 0, 1), ("X", 4, 2), ("S", 2, 3), ("L", 5),
+    ("XF", 3, 2), ("X", 3, 1), ("L", 4), ("S", 0, 5), ("XF", 4, 0), ("S", 0, 4), ("H", 3, 3), ("X", 4, 1),
+    ("XF", 4, 2), ("H", 1, 5), ("S", 3, 3), ("X", 1, 3), ("S", 1, 5), ("H", 1, 4), ("X", 0, 5), ("XF", 3, 1),
+    ("S", 1, 4), ("H", 4, 3), ("X", 0, 4), ("FI", 1, 0), ("H", 2, 5), ("S", 4, 3), ("XF", 4, 1), ("X", 2, 3),
+    ("FI", 1, 2), ("H", 2, 4), ("S", 2, 5), ("S", 2, 4), ("XF", 1, 3), ("H", 3, 5), ("XF", 0, 5), ("S", 3, 5),
+    ("X", 1, 5), ("X", 3, 3), ("XF", 0, 4), ("FI", 1, 1), ("XF", 2, 3), ("H", 3, 4), ("X", 4, 3), ("H", 4, 5),
+    ("S", 3, 4), ("XF", 1, 5), ("X", 1, 4), ("S", 4, 5), ("X", 2, 5), ("XF", 3, 3), ("H", 4, 4), ("FI", 0, 3),
+    ("S", 4, 4), ("X", 2, 4), ("XF", 4, 3), ("X", 3, 5), ("XF", 1, 4), ("XF", 2, 5), ("X", 4, 5), ("XF", 2, 4),
+    ("X", 3, 4), ("FI", 1, 3), ("XF", 3, 5), ("FI", 0, 5), ("X", 4, 4), ("XF", 4, 5), ("FI", 0, 4), ("FM", 0),
+    ("FO", 0, 0), ("O", 2, 0), ("FO", 0, 1), ("O", 1, 1), ("FO", 0, 2), ("XF", 3, 4), ("FO", 0, 3), ("FO", 0, 4),
+    ("FO", 0, 5), ("O", 2, 4), ("XF", 4, 4), ("FI", 1, 5), ("O", 2, 1), ("M", 2, 0), ("M", 1, 1), ("M", 2, 4),
+    ("FI", 1, 4), ("FM", 1), ("FO", 1, 0), ("FO", 1, 1), ("O", 4, 0), ("FO", 1, 2), ("M", 2, 1), ("FO", 1, 4),
+    ("FO", 1, 5), ("N", 2, 0), ("FO", 1, 3), ("O", 4, 5), ("O", 3, 0), ("N", 1, 1), ("G", 2, 1), ("G", 3, 1),
+    ("O", 4, 1), ("N", 2, 4), ("M", 4, 0), ("N", 2, 1), ("M", 4, 5), ("O", 3, 1), ("M", 3, 0), ("M", 4, 1),
+    ("N", 4, 0), ("N", 4, 5), ("M", 3, 1), ("N", 3, 0), ("O", 3, 5), ("O", 4, 4), ("O", 3, 2), ("N", 4, 1),
+    ("O", 3, 4), ("O", 4, 3), ("N", 3, 1), ("M", 3, 5), ("G", 4, 0), ("M", 4, 4), ("M", 3, 2), ("M", 3, 4),
+    ("P", 4, 0), ("M", 4, 3), ("N", 3, 5), ("G", 4, 1), ("N", 4, 4), ("P", 4, 1), ("O", 4, 2), ("N", 3, 2),
+    ("O", 3, 3), ("N", 3, 4), ("O", 2, 5), ("O", 1, 4), ("O", 2, 2), ("N", 4, 3), ("O", 2, 3), ("M", 4, 2),
+    ("P", 3, 1), ("M", 3, 3), ("M", 2, 5), ("M", 1, 4), ("M", 2, 2), ("M", 2, 3), ("G", 4, 4), ("N", 4, 2),
+    ("P", 4, 4), ("N", 3, 3), ("N", 2, 5), ("G", 4, 5), ("P", 2, 1), ("O", 1, 5), ("O", 1, 2), ("N", 1, 4),
+    ("G", 3, 4), ("P", 4, 5), ("G", 2, 4), ("O", 1, 3), ("N", 2, 2), ("O", 1, 0), ("N", 2, 3), ("M", 1, 5),
+    ("P", 3, 4), ("G", 4, 2), ("M", 1, 2), ("G", 4, 3), ("P", 4, 2), ("M", 1, 3), ("M", 1, 0), ("P", 4, 3),
+    ("N", 1, 5), ("G", 3, 5), ("G", 2, 5), ("P", 3, 5), ("P", 2, 4), ("N", 1, 2), ("G", 2, 2), ("G", 3, 2),
+    ("O", 0, 0), ("O", 0, 1), ("N", 1, 3), ("G", 3, 3), ("G", 2, 3), ("P", 3, 2), ("O", 0, 2), ("O", 0, 3),
+    ("N", 1, 0), ("G", 2, 0), ("P", 3, 3), ("G", 3, 0), ("P", 2, 5), ("M", 0, 0), ("M", 0, 1), ("P", 3, 0),
+    ("M", 0, 2), ("M", 0, 3), ("P", 2, 2), ("N", 0, 0), ("G", 0, 0), ("G", 1, 0), ("P", 2, 3), ("O", 0, 5),
+    ("N", 0, 1), ("G", 1, 1), ("G", 0, 1), ("O", 0, 4), ("N", 0, 2), ("G", 1, 2), ("P", 1, 1), ("G", 0, 2),
+    ("P", 2, 0), ("N", 0, 3), ("G", 1, 3), ("G", 0, 3), ("M", 0, 5), ("M", 0, 4), ("P", 1, 2), ("P", 1, 3),
+    ("N", 0, 5), ("G", 0, 5), ("G", 1, 5), ("E", 1), ("N", 0, 4), ("G", 0, 4), ("G", 1, 4), ("P", 1, 5), ("P", 1, 0),
+    ("P", 1, 4), ("E", 2), ("E", 3), ("E", 5), ("E", 0), ("E", 4),
 ]
 
 
@@ -367,10 +367,17 @@
     go(p_meta, 0)
     run = {"L": launch, "H": hop, "S": choose, "X": spread, "XF": forward, "FI": layer_in, "FM": layer_mid,
            "FO": layer_out, "O": begin, "M": middle, "N": finish, "G": give, "P": pass_on, "E": last}
-    for task in ORDER:
+    first_out = [t[0] for t in ORDER].index("FO")
+    early = 0
+    for n, task in enumerate(ORDER):
+        if n == first_out:
+            early = len(sent)
+        if task[0] == "E" and new("early"):
+            for make, a in sent[:early]:
+                make(*a).wait_send()
         with jax.named_scope("_".join(map(str, task))):
             run[task[0]](*task[1:])
-    for make, a in sent:
+    for make, a in sent[early:]:
         make(*a).wait_send()
 
 

time: 173 us -> 172 us (level)
  no operation moved by 1% of the time
where the time goes in v6:
time: 172 us
  Pallas kernels  170 us (99%)
  local copies, waits for them, and re-layouts  1.77 us (1%)
    pallas_call x1, Pallas kernels, on_device(): pl.pallas_call(functools.partial(kernel, E, NX, rows, width), out_shape=j...  170 us

profile of v6, /device:TPU:33, one launch (start us, length us, event | category | flops | bytes accessed | tf_op | source)
XLA Modules:
  0.0 172.1 jit_solution(12850900481857828139)
XLA Ops:
  0.0 170.4 %shard_map.73 = bf16[32,6144]{1,0:T(8,128)(2,1)} custom-call(bf16[32,6144]{1,0:T(8,128)(2,1)} %tokens.1, s32[2,32]{1,0:T(2,128)} %bitcast.4, f32[2,32]{1,0:T(2,128)} %bitcast.5, f32[1,6144]{1,0:T(1,128)} %bitcast.3, bf16[1,6144,256]{2,1,0:T(8,128)(2,1)} %wg_in.1, bf16[1,6144,256]{2,1,0:T(8,128)(2,1)} %wu_in.1, bf16[1,256,6144]{2,1,0:T(8,128)(2,1)} %wd_in.1), custom_call_target="tpu_custom_call" | custom-call | tf_op jit(solution)/shard_map/pallas_call | solution.py:391
  170.4 1.8 %copy.9 = bf16[32,6144]{1,0:T(8,128)(2,1)} copy(bf16[32,6144]{1,0:T(8,128)(2,1)} %shard_map.73) | data formatting | bytes 786432
